TPU v7x, 256 devices: a 4x2x16 block of a 4x16x16 slice. The times are simulated.
256 devices in a mesh: parts: 2 (over y), gz: 32 (over z, core), shot: 4 (over x).
Axes of the slice: x: 4, y: 2, z: 16, core: 2. Of those that a mesh axis runs over, the one named last changes fastest.
The devices are a block of a 4x16x16 slice.
Arguments:
- wavefields: float32 [8, 2, 9, 128, 32, 128], P(('parts', 'shot'), None, None, 'gz'), parts along dimension 0, may hold values from -6 to 6
- earth_model: float32 [6, 128, 32, 128], P('parts', 'gz'), parts along dimension 0, may hold values from 0.4 to 1.6
- source_depth: int32 [8], P(('parts', 'shot')), parts along dimension 0, may hold values from 0 to 127
- source_column: int32 [8], P(('parts', 'shot')), parts along dimension 0, may hold values from 0 to 4095
- wavelet: float32 [8, 8], P(('parts', 'shot')), parts along dimension 0, may hold values from -30 to 30
- receiver_depth: int32 [8, 64], P(('parts', 'shot')), parts along dimension 0, may hold values from 0 to 127
- receiver_column: int32 [8, 64], P(('parts', 'shot')), parts along dimension 0, may hold values from 0 to 4095
- traces: float32 [8, 8, 64], P(('parts', 'shot')), parts along dimension 0, may hold values from -30 to 30
Outputs:
- images: float32 [4, 128, 32, 128], P('parts', 'gz'), parts along dimension 0
There are 2 independent parts, one for each index of `parts`. A program takes and returns all parts, laid end to end along the dimension named above; each array names one. Nothing has to cross between parts.
All inputs are finite; a program needn't handle non-finite values.
Results may differ from a plain program's by a relative error of at most 0.00002.
Values sent between devices are 32-bit elements; how exact they have to be, the bound alone decides.
No kernel may reach another device: no remote copies, remote signals or barrier semaphores. Data moves between devices by JAX's collectives and lax.ppermute only.
A program may use at most 64 MiB of HBM per device.

v0:
```python
import jax
import jax.numpy as jnp
from jax import lax
from jax.sharding import PartitionSpec as P

time_step = 0.15


def shifted(value, axis, steps):
    count = lax.axis_size(axis)
    first, last = (max(0, -steps), min(count, count - steps))
    return lax.ppermute(value, axis, [(source, source + steps) for source in range(first, last)])


def copy_for_each(value, axis):
    size = lax.axis_size(axis)
    return lax.all_to_all(
        jnp.broadcast_to(value[None], (size, *value.shape)), axis, 0, 0, tiled=True
    )


def of_everyone(value, axis):
    everything = copy_for_each(value, axis)
    return jnp.sum(everything, axis=0)


def together(arrays, axis):
    line, at, outs = (jnp.concatenate([a.reshape(-1) for a in arrays]), 0, [])
    total = of_everyone(line, axis)
    for a in arrays:
        outs.append(total[at : at + a.size].reshape(a.shape))
        at += a.size
    return tuple(outs)


def forward_diff(array, dim_index):
    length = array.shape[dim_index]
    following = jnp.concatenate(
        [
            lax.slice_in_dim(array, 1, length, axis=dim_index),
            jnp.zeros_like(lax.slice_in_dim(array, 0, 1, axis=dim_index)),
        ],
        axis=dim_index,
    )
    return following - array


def backward_diff(array, dim_index):
    length = array.shape[dim_index]
    previous = jnp.concatenate(
        [
            jnp.zeros_like(lax.slice_in_dim(array, 0, 1, axis=dim_index)),
            lax.slice_in_dim(array, 0, length - 1, axis=dim_index),
        ],
        axis=dim_index,
    )
    return array - previous


def depth_forward(array, plane_high):
    following = jnp.concatenate([array[:, 1:], plane_high[:, None]], axis=1)
    return following - array


def depth_backward(array, plane_low):
    previous = jnp.concatenate([plane_low[:, None], array[:, :-1]], axis=1)
    return array - previous


def velocity_half(fields, buoyancy, sxz_low, syz_low, szz_high):
    vel_x, vel_y, vel_z, sig_xx, sig_yy, sig_zz, sig_xy, sig_xz, sig_yz = fields
    vel_x = vel_x + time_step * buoyancy * (
        forward_diff(sig_xx, 2) + backward_diff(sig_xy, 3) + depth_backward(sig_xz, sxz_low)
    )
    vel_y = vel_y + time_step * buoyancy * (
        backward_diff(sig_xy, 2) + forward_diff(sig_yy, 3) + depth_backward(sig_yz, syz_low)
    )
    vel_z = vel_z + time_step * buoyancy * (
        backward_diff(sig_xz, 2) + backward_diff(sig_yz, 3) + depth_forward(sig_zz, szz_high)
    )
    return (vel_x, vel_y, vel_z)


def stress_half(fields, lame_lambda, shear_mu, vz_low, vx_high, vy_high):
    vel_x, vel_y, vel_z, sig_xx, sig_yy, sig_zz, sig_xy, sig_xz, sig_yz = fields
    strain_x = backward_diff(vel_x, 2)
    strain_y = backward_diff(vel_y, 3)
    strain_z = depth_backward(vel_z, vz_low)
    spread = strain_x + strain_y + strain_z
    sig_xx = sig_xx + time_step * (lame_lambda * spread + 2.0 * shear_mu * strain_x)
    sig_yy = sig_yy + time_step * (lame_lambda * spread + 2.0 * shear_mu * strain_y)
    sig_zz = sig_zz + time_step * (lame_lambda * spread + 2.0 * shear_mu * strain_z)
    vx_up = depth_forward(vel_x, vx_high)
    vy_up = depth_forward(vel_y, vy_high)
    vz_along_x = forward_diff(vel_z, 2)
    vz_along_y = forward_diff(vel_z, 3)
    vx_along_y = forward_diff(vel_x, 3)
    vy_along_x = forward_diff(vel_y, 2)
    sig_xy = sig_xy + time_step * shear_mu * (vx_along_y + vy_along_x)
    sig_xz = sig_xz + time_step * shear_mu * (vx_up + vz_along_x)
    sig_yz = sig_yz + time_step * shear_mu * (vy_up + vz_along_y)
    rotation = vz_along_y - vy_up + (vx_up - vz_along_x) + (vy_along_x - vx_along_y)
    return ([vel_x, vel_y, vel_z, sig_xx, sig_yy, sig_zz, sig_xy, sig_xz, sig_yz], rotation)


def add_points(field_in, wave_index, depth_at, row_index, col_index, amounts, limit_at):
    inside = (depth_at >= 0) & (depth_at < limit_at)
    place_at = jnp.where(inside, depth_at, limit_at)
    return field_in.at[wave_index, place_at, row_index, col_index].add(amounts, mode="drop")


def advance(fields, material, receiver_add, source_add):
    stress_lows = shifted(jnp.stack([fields[7][:, -1], fields[8][:, -1]]), "gz", 1)
    sxz_low = stress_lows[0]
    syz_low = stress_lows[1]
    szz_high = shifted(fields[5][:, 0], "gz", -1)
    vel_x, vel_y, vel_z = velocity_half(fields, material[0], sxz_low, syz_low, szz_high)
    vel_z = receiver_add(vel_z)
    vz_low = shifted(vel_z[:, -1], "gz", 1)
    vel_highs = shifted(jnp.stack([vel_x[:, 0], vel_y[:, 0]]), "gz", -1)
    vx_high = vel_highs[0]
    vy_high = vel_highs[1]
    updated, rotation = stress_half(
        [vel_x, vel_y, vel_z] + list(fields[3:]), material[1], material[2], vz_low, vx_high, vy_high
    )
    for field_no in (3, 4, 5):
        updated[field_no] = source_add(updated[field_no])
    return (updated, rotation)


def on_device(
    wavefields,
    earth_model,
    source_depth,
    source_column,
    wavelet,
    receiver_depth,
    receiver_column,
    traces,
):
    fields_now = wavefields[0]
    slab_depth = fields_now.shape[2]
    width_y = fields_now.shape[4]
    steps_total = wavelet.shape[1]
    offset = lax.axis_index("gz") * slab_depth
    src_row = source_column[0] // width_y
    src_col = source_column[0] % width_y
    rec_row = receiver_column[0] // width_y
    rec_col = receiver_column[0] % width_y
    tallies = {
        "image_pp": jnp.zeros(fields_now.shape[2:], jnp.float32),
        "image_ps": jnp.zeros(fields_now.shape[2:], jnp.float32),
        "first_half": None,
    }

    def tally(step_index, pressure, rotation):
        tallies["image_pp"] = tallies["image_pp"] + pressure[0] * pressure[1]
        tallies["image_ps"] = tallies["image_ps"] + pressure[0] * rotation[1]
        if step_index == steps_total // 2 - 1:
            tallies["first_half"] = together((tallies["image_pp"], tallies["image_ps"]), "shot")
            tallies["image_pp"] = jnp.zeros_like(tallies["image_pp"])
            tallies["image_ps"] = jnp.zeros_like(tallies["image_ps"])

    def injectors(step_index, limit_at):

        def receiver_add(vel_z):
            return add_points(
                vel_z,
                1,
                receiver_depth[0] - offset,
                rec_row,
                rec_col,
                time_step * traces[0, step_index],
                limit_at,
            )

        def source_add(normal):
            return add_points(
                normal,
                0,
                source_depth[0] - offset,
                src_row,
                src_col,
                time_step * wavelet[0, step_index],
                limit_at,
            )

        return (receiver_add, source_add)

    fields = [fields_now[:, field_no] for field_no in range(9)]
    for step_index in range(steps_total):
        receiver_add, source_add = injectors(step_index, slab_depth)
        fields, rotation = advance(fields, earth_model, receiver_add, source_add)
        pressure = (fields[3] + fields[4] + fields[5]) / 3.0
        tally(step_index, pressure, rotation)
    summed_pp, summed_ps = together((tallies["image_pp"], tallies["image_ps"]), "shot")
    summed_pp = summed_pp + tallies["first_half"][0]
    summed_ps = summed_ps + tallies["first_half"][1]
    return jnp.stack([summed_pp, summed_ps]) / steps_total


def solution(mesh):
    placed = (
        P(("parts", "shot"), None, None, "gz", None, None),
        P("parts", "gz", None, None),
        P(("parts", "shot")),
        P(("parts", "shot")),
        P(("parts", "shot"), None),
        P(("parts", "shot"), None),
        P(("parts", "shot"), None),
        P(("parts", "shot"), None, None),
    )
    return jax.shard_map(
        on_device,
        mesh=mesh,
        in_specs=placed,
        out_specs=P("parts", "gz", None, None),
        check_vma=False,
    )
```

profile of v0, /device:TPU:33, one launch (start us, length us, event | category | flops | bytes accessed | tf_op | source)
XLA Modules:
  0.0 278.3 jit_solution(14094540140864914330)
XLA Ops:
  1.6 5.7 %collective-permute-start = (f32[2,2,32,128]{3,2,1,0:T(8,128)S(1)}, f32[2,2,32,128]{3,2,1,0:T(8,128)S(1)}, u32[]{:S(2)}, u32[]{:S(2)}) collective-permute-start(f32[2,2,32,128]{3,2,1,0:T(8,128)S(1)} %pad_maximum_fusion.4), channel_id=1, source_target_pairs={{0,4},{4,8},{8,12},{12,16},{16,20},{20,24},{24,28},{28,32},{32,36}... | collective-permute-start | bytes 196616 | tf_op jit(solution)/shard_map/ppermute | solution.py:12
  7.3 17.9 %collective-permute-start.1 = (f32[2,32,128]{2,1,0:T(8,128)S(1)}, f32[2,32,128]{2,1,0:T(8,128)S(1)}, u32[]{:S(2)}, u32[]{:S(2)}) collective-permute-start(f32[2,32,128]{2,1,0:T(8,128)S(1)} %slice_bitcast_fusion.85), channel_id=1, source_target_pairs={{4,0},{8,4},{12,8},{16,12},{20,16},{24,20},{28,24},{32,28},{36,32}... | collective-permute-start | bytes 98312 | tf_op jit(solution)/shard_map/ppermute | solution.py:12
  35.7 5.3 %scatter_fusion = f32[2,4,32,128]{3,2,1,0:T(8,128)S(1)} fusion(f32[2,4,32,128]{3,2,1,0:T(8,128)S(1)} %copy.495, s32[64]{0:T(128)S(1)} %fusion.123, f32[64]{0:T(128)S(1)} %get-tuple-element.513), kind=kCustom, calls=%fused_computation | custom fusion | flops 64 | bytes 1792 | tf_op jit(solution)/shard_map/scatter-add | solution.py:109
  41.3 3.7 %collective-permute-start.2 = (f32[2,32,128]{2,1,0:T(8,128)S(1)}, f32[2,32,128]{2,1,0:T(8,128)S(1)}, u32[]{:S(2)}, u32[]{:S(2)}) collective-permute-start(f32[2,32,128]{2,1,0:T(8,128)S(1)} %slice_bitcast_fusion.84), channel_id=1, source_target_pairs={{0,4},{4,8},{8,12},{12,16},{16,20},{20,24},{24,28},{28,32},{32,36}... | collective-permute-start | bytes 98312 | tf_op jit(solution)/shard_map/ppermute | solution.py:12
  47.1 4.3 %collective-permute-start.4 = (f32[2,2,32,128]{3,2,1,0:T(8,128)S(1)}, f32[2,2,32,128]{3,2,1,0:T(8,128)S(1)}, u32[]{:S(2)}, u32[]{:S(2)}) collective-permute-start(f32[2,2,32,128]{3,2,1,0:T(8,128)S(1)} %pad_maximum_fusion.6), channel_id=1, source_target_pairs={{0,4},{4,8},{8,12},{12,16},{16,20},{20,24},{24,28},{28,32},{32,36}... | collective-permute-start | bytes 196616 | tf_op jit(solution)/shard_map/ppermute | solution.py:12
  64.7 5.3 %scatter_fusion.1 = f32[2,4,32,128]{3,2,1,0:T(8,128)S(1)} fusion(f32[2,4,32,128]{3,2,1,0:T(8,128)S(1)} %get-tuple-element.468, s32[64]{0:T(128)S(1)} %fusion.123, f32[64]{0:T(128)S(1)} %get-tuple-element.512), kind=kCustom, calls=%fused_computation.1 | custom fusion | flops 64 | bytes 1792 | tf_op jit(solution)/shard_map/scatter-add | solution.py:109
  83.4 4.3 %collective-permute-start.8 = (f32[2,2,32,128]{3,2,1,0:T(8,128)S(1)}, f32[2,2,32,128]{3,2,1,0:T(8,128)S(1)}, u32[]{:S(2)}, u32[]{:S(2)}) collective-permute-start(f32[2,2,32,128]{3,2,1,0:T(8,128)S(1)} %pad_maximum_fusion.8), channel_id=1, source_target_pairs={{0,4},{4,8},{8,12},{12,16},{16,20},{20,24},{24,28},{28,32},{32,36}... | collective-permute-start | bytes 196616 | tf_op jit(solution)/shard_map/ppermute | solution.py:12
  90.6 5.3 %scatter_fusion.2 = f32[2,4,32,128]{3,2,1,0:T(8,128)S(1)} fusion(f32[2,4,32,128]{3,2,1,0:T(8,128)S(1)} %copy.539, s32[64]{0:T(128)S(1)} %fusion.123, f32[64]{0:T(128)S(1)} %get-tuple-element.511), kind=kCustom, calls=%fused_computation.2 | custom fusion | flops 64 | bytes 1792 | tf_op jit(solution)/shard_map/scatter-add | solution.py:109
  122.7 5.3 %scatter_fusion.3 = f32[2,4,32,128]{3,2,1,0:T(8,128)S(1)} fusion(f32[2,4,32,128]{3,2,1,0:T(8,128)S(1)} %copy.572, s32[64]{0:T(128)S(1)} %fusion.123, f32[64]{0:T(128)S(1)} %get-tuple-element.510), kind=kCustom, calls=%fused_computation.3 | custom fusion | flops 64 | bytes 1792 | tf_op jit(solution)/shard_map/scatter-add | solution.py:109
  128.4 3.7 %collective-permute-start.14 = (f32[2,32,128]{2,1,0:T(8,128)S(1)}, f32[2,32,128]{2,1,0:T(8,128)S(1)}, u32[]{:S(2)}, u32[]{:S(2)}) collective-permute-start(f32[2,32,128]{2,1,0:T(8,128)S(1)} %slice_bitcast_fusion.54), channel_id=1, source_target_pairs={{0,4},{4,8},{8,12},{12,16},{16,20},{20,24},{24,28},{28,32},{32,36}... | collective-permute-start | bytes 98312 | tf_op jit(solution)/shard_map/ppermute | solution.py:12
  134.1 4.3 %collective-permute-start.16 = (f32[2,2,32,128]{3,2,1,0:T(8,128)S(1)}, f32[2,2,32,128]{3,2,1,0:T(8,128)S(1)}, u32[]{:S(2)}, u32[]{:S(2)}) collective-permute-start(f32[2,2,32,128]{3,2,1,0:T(8,128)S(1)} %pad_maximum_fusion.12), channel_id=1, source_target_pairs={{0,4},{4,8},{8,12},{12,16},{16,20},{20,24},{24,28},{28,32},{32,36}... | collective-permute-start | bytes 196616 | tf_op jit(solution)/shard_map/ppermute | solution.py:12
  149.4 5.3 %scatter_fusion.4 = f32[2,4,32,128]{3,2,1,0:T(8,128)S(1)} fusion(f32[2,4,32,128]{3,2,1,0:T(8,128)S(1)} %copy.608, s32[64]{0:T(128)S(1)} %fusion.123, f32[64]{0:T(128)S(1)} %get-tuple-element.509), kind=kCustom, calls=%fused_computation.4 | custom fusion | flops 64 | bytes 1792 | tf_op jit(solution)/shard_map/scatter-add | solution.py:109
  157.1 3.7 %collective-permute-start.18 = (f32[2,32,128]{2,1,0:T(8,128)S(1)}, f32[2,32,128]{2,1,0:T(8,128)S(1)}, u32[]{:S(2)}, u32[]{:S(2)}) collective-permute-start(f32[2,32,128]{2,1,0:T(8,128)S(1)} %slice_bitcast_fusion.44), channel_id=1, source_target_pairs={{0,4},{4,8},{8,12},{12,16},{16,20},{20,24},{24,28},{28,32},{32,36}... | collective-permute-start | bytes 98312 | tf_op jit(solution)/shard_map/ppermute | solution.py:12
  166.3 3.6 %all-to-all-start.1 = ((f32[4,1,32768]{2,1,0:T(1,128)}), f32[4,1,32768]{2,1,0:T(1,128)S(1)}, u32[]{:S(2)}, u32[]{:S(2)}) async-start(f32[4,1,32768]{2,1,0:T(1,128)} %broadcast_in_dim.71), calls=%async_computation.1 | async-start | bytes 1048576 | tf_op jit(solution)/shard_map/all_to_all | solution.py:17
  172.4 4.3 %collective-permute-start.20 = (f32[2,2,32,128]{3,2,1,0:T(8,128)S(1)}, f32[2,2,32,128]{3,2,1,0:T(8,128)S(1)}, u32[]{:S(2)}, u32[]{:S(2)}) collective-permute-start(f32[2,2,32,128]{3,2,1,0:T(8,128)S(1)} %pad_maximum_fusion.14), channel_id=1, source_target_pairs={{0,4},{4,8},{8,12},{12,16},{16,20},{20,24},{24,28},{28,32},{32,36}... | collective-permute-start | bytes 196616 | tf_op jit(solution)/shard_map/ppermute | solution.py:12
  184.0 5.3 %scatter_fusion.5 = f32[2,4,32,128]{3,2,1,0:T(8,128)S(1)} fusion(f32[2,4,32,128]{3,2,1,0:T(8,128)S(1)} %copy.642, s32[64]{0:T(128)S(1)} %fusion.123, f32[64]{0:T(128)S(1)} %get-tuple-element.508), kind=kCustom, calls=%fused_computation.5 | custom fusion | flops 64 | bytes 1792 | tf_op jit(solution)/shard_map/scatter-add | solution.py:109
  191.7 3.7 %collective-permute-start.22 = (f32[2,32,128]{2,1,0:T(8,128)S(1)}, f32[2,32,128]{2,1,0:T(8,128)S(1)}, u32[]{:S(2)}, u32[]{:S(2)}) collective-permute-start(f32[2,32,128]{2,1,0:T(8,128)S(1)} %slice_bitcast_fusion.34), channel_id=1, source_target_pairs={{0,4},{4,8},{8,12},{12,16},{16,20},{20,24},{24,28},{28,32},{32,36}... | collective-permute-start | bytes 98312 | tf_op jit(solution)/shard_map/ppermute | solution.py:12
  201.0 4.3 %collective-permute-start.24 = (f32[2,2,32,128]{3,2,1,0:T(8,128)S(1)}, f32[2,2,32,128]{3,2,1,0:T(8,128)S(1)}, u32[]{:S(2)}, u32[]{:S(2)}) collective-permute-start(f32[2,2,32,128]{3,2,1,0:T(8,128)S(1)} %pad_maximum_fusion.16), channel_id=1, source_target_pairs={{0,4},{4,8},{8,12},{12,16},{16,20},{20,24},{24,28},{28,32},{32,36}... | collective-permute-start | bytes 196616 | tf_op jit(solution)/shard_map/ppermute | solution.py:12
  213.0 5.3 %scatter_fusion.6 = f32[2,4,32,128]{3,2,1,0:T(8,128)S(1)} fusion(f32[2,4,32,128]{3,2,1,0:T(8,128)S(1)} %copy.679, s32[64]{0:T(128)S(1)} %fusion.123, f32[64]{0:T(128)S(1)} %get-tuple-element.514), kind=kCustom, calls=%fused_computation.6 | custom fusion | flops 64 | bytes 1792 | tf_op jit(solution)/shard_map/scatter-add | solution.py:109
  218.3 3.7 %collective-permute-start.26 = (f32[2,32,128]{2,1,0:T(8,128)S(1)}, f32[2,32,128]{2,1,0:T(8,128)S(1)}, u32[]{:S(2)}, u32[]{:S(2)}) collective-permute-start(f32[2,32,128]{2,1,0:T(8,128)S(1)} %slice_bitcast_fusion.24), channel_id=1, source_target_pairs={{0,4},{4,8},{8,12},{12,16},{16,20},{20,24},{24,28},{28,32},{32,36}... | collective-permute-start | bytes 98312 | tf_op jit(solution)/shard_map/ppermute | solution.py:12
  232.4 3.7 %collective-permute-start.28 = (f32[2,2,32,128]{3,2,1,0:T(8,128)S(1)}, f32[2,2,32,128]{3,2,1,0:T(8,128)S(1)}, u32[]{:S(2)}, u32[]{:S(2)}) collective-permute-start(f32[2,2,32,128]{3,2,1,0:T(8,128)S(1)} %pad_maximum_fusion.18), channel_id=1, source_target_pairs={{0,4},{4,8},{8,12},{12,16},{16,20},{20,24},{24,28},{28,32},{32,36}... | collective-permute-start | bytes 196616 | tf_op jit(solution)/shard_map/ppermute | solution.py:12
  241.9 5.3 %scatter_fusion.7 = f32[2,4,32,128]{3,2,1,0:T(8,128)S(1)} fusion(f32[2,4,32,128]{3,2,1,0:T(8,128)S(1)} %get-tuple-element.413, s32[64]{0:T(128)S(1)} %fusion.123, f32[64]{0:T(128)S(1)} %get-tuple-element.507), kind=kCustom, calls=%fused_computation.7 | custom fusion | flops 64 | bytes 1792 | tf_op jit(solution)/shard_map/scatter-add | solution.py:109
  262.8 4.4 %all-to-all-start = ((f32[4,1,32768]{2,1,0:T(1,128)}), f32[4,1,32768]{2,1,0:T(1,128)S(1)}, u32[]{:S(2)}, u32[]{:S(2)}) async-start(f32[4,1,32768]{2,1,0:T(1,128)} %broadcast_in_dim.70), calls=%async_computation | async-start | bytes 1048576 | tf_op jit(solution)/shard_map/all_to_all | solution.py:17
  267.6 9.4 %all-to-all-done = f32[4,1,32768]{2,1,0:T(1,128)S(1)} async-done(((f32[4,1,32768]{2,1,0:T(1,128)}), f32[4,1,32768]{2,1,0:T(1,128)S(1)}, u32[]{:S(2)}, u32[]{:S(2)}) %all-to-all-start) | async-done | bytes 524320 | tf_op jit(solution)/shard_map/all_to_all | solution.py:17
  (428 shorter events, 98.3 us)
Async XLA Ops:
  1.6 31.7 %collective-permute-start = (f32[2,2,32,128]{3,2,1,0:T(8,128)S(1)}, f32[2,2,32,128]{3,2,1,0:T(8,128)S(1)}, u32[]{:S(2)}, u32[]{:S(2)}) collective-permute-start(f32[2,2,32,128]{3,2,1,0:T(8,128)S(1)} %pad_maximum_fusion.4), channel_id=1, source_target_pairs={{0,4},{4,8},{8,12},{12,16},{16,20},{20,24},{24,28},{28,32},{32,36}... | collective-permute-start | bytes 196616 | tf_op jit(solution)/shard_map/ppermute | solution.py:12
  7.3 26.0 %collective-permute-start.1 = (f32[2,32,128]{2,1,0:T(8,128)S(1)}, f32[2,32,128]{2,1,0:T(8,128)S(1)}, u32[]{:S(2)}, u32[]{:S(2)}) collective-permute-start(f32[2,32,128]{2,1,0:T(8,128)S(1)} %slice_bitcast_fusion.85), channel_id=1, source_target_pairs={{4,0},{8,4},{12,8},{16,12},{20,16},{24,20},{28,24},{32,28},{36,32}... | collective-permute-start | bytes 98312 | tf_op jit(solution)/shard_map/ppermute | solution.py:12
  33.7 11.3 %collective-permute-start.3 = (f32[2,2,32,128]{3,2,1,0:T(8,128)S(1)}, f32[2,2,32,128]{3,2,1,0:T(8,128)S(1)}, u32[]{:S(2)}, u32[]{:S(2)}) collective-permute-start(f32[2,2,32,128]{3,2,1,0:T(8,128)S(1)} %pad_maximum_fusion.5), channel_id=1, source_target_pairs={{4,0},{8,4},{12,8},{16,12},{20,16},{24,20},{28,24},{32,28},{36,32}... | collective-permute-start | bytes 196616 | tf_op jit(solution)/shard_map/ppermute | solution.py:12
  47.1 14.2 %collective-permute-start.4 = (f32[2,2,32,128]{3,2,1,0:T(8,128)S(1)}, f32[2,2,32,128]{3,2,1,0:T(8,128)S(1)}, u32[]{:S(2)}, u32[]{:S(2)}) collective-permute-start(f32[2,2,32,128]{3,2,1,0:T(8,128)S(1)} %pad_maximum_fusion.6), channel_id=1, source_target_pairs={{0,4},{4,8},{8,12},{12,16},{16,20},{20,24},{24,28},{28,32},{32,36}... | collective-permute-start | bytes 196616 | tf_op jit(solution)/shard_map/ppermute | solution.py:12
  61.6 11.4 %collective-permute-start.7 = (f32[2,2,32,128]{3,2,1,0:T(8,128)S(1)}, f32[2,2,32,128]{3,2,1,0:T(8,128)S(1)}, u32[]{:S(2)}, u32[]{:S(2)}) collective-permute-start(f32[2,2,32,128]{3,2,1,0:T(8,128)S(1)} %pad_maximum_fusion.7), channel_id=1, source_target_pairs={{4,0},{8,4},{12,8},{16,12},{20,16},{24,20},{28,24},{32,28},{36,32}... | collective-permute-start | bytes 196616 | tf_op jit(solution)/shard_map/ppermute | solution.py:12
  78.6 11.9 %collective-permute-start.9 = (f32[2,32,128]{2,1,0:T(8,128)S(1)}, f32[2,32,128]{2,1,0:T(8,128)S(1)}, u32[]{:S(2)}, u32[]{:S(2)}) collective-permute-start(f32[2,32,128]{2,1,0:T(8,128)S(1)} %slice_bitcast_fusion.65), channel_id=1, source_target_pairs={{4,0},{8,4},{12,8},{16,12},{20,16},{24,20},{28,24},{32,28},{36,32}... | collective-permute-start | bytes 98312 | tf_op jit(solution)/shard_map/ppermute | solution.py:12
  83.4 15.2 %collective-permute-start.8 = (f32[2,2,32,128]{3,2,1,0:T(8,128)S(1)}, f32[2,2,32,128]{3,2,1,0:T(8,128)S(1)}, u32[]{:S(2)}, u32[]{:S(2)}) collective-permute-start(f32[2,2,32,128]{3,2,1,0:T(8,128)S(1)} %pad_maximum_fusion.8), channel_id=1, source_target_pairs={{0,4},{4,8},{8,12},{12,16},{16,20},{20,24},{24,28},{28,32},{32,36}... | collective-permute-start | bytes 196616 | tf_op jit(solution)/shard_map/ppermute | solution.py:12
  106.1 10.9 %collective-permute-start.12 = (f32[2,2,32,128]{3,2,1,0:T(8,128)S(1)}, f32[2,2,32,128]{3,2,1,0:T(8,128)S(1)}, u32[]{:S(2)}, u32[]{:S(2)}) collective-permute-start(f32[2,2,32,128]{3,2,1,0:T(8,128)S(1)} %pad_maximum_fusion.10), channel_id=1, source_target_pairs={{0,4},{4,8},{8,12},{12,16},{16,20},{20,24},{24,28},{28,32},{32,36}... | collective-permute-start | bytes 196616 | tf_op jit(solution)/shard_map/ppermute | solution.py:12
  120.6 11.5 %collective-permute-start.15 = (f32[2,2,32,128]{3,2,1,0:T(8,128)S(1)}, f32[2,2,32,128]{3,2,1,0:T(8,128)S(1)}, u32[]{:S(2)}, u32[]{:S(2)}) collective-permute-start(f32[2,2,32,128]{3,2,1,0:T(8,128)S(1)} %pad_maximum_fusion.11), channel_id=1, source_target_pairs={{4,0},{8,4},{12,8},{16,12},{20,16},{24,20},{28,24},{32,28},{36,32}... | collective-permute-start | bytes 196616 | tf_op jit(solution)/shard_map/ppermute | solution.py:12
  134.1 20.6 %collective-permute-start.16 = (f32[2,2,32,128]{3,2,1,0:T(8,128)S(1)}, f32[2,2,32,128]{3,2,1,0:T(8,128)S(1)}, u32[]{:S(2)}, u32[]{:S(2)}) collective-permute-start(f32[2,2,32,128]{3,2,1,0:T(8,128)S(1)} %pad_maximum_fusion.12), channel_id=1, source_target_pairs={{0,4},{4,8},{8,12},{12,16},{16,20},{20,24},{24,28},{28,32},{32,36}... | collective-permute-start | bytes 196616 | tf_op jit(solution)/shard_map/ppermute | solution.py:12
  141.8 7.4 %collective-permute-start.17 = (f32[2,32,128]{2,1,0:T(8,128)S(1)}, f32[2,32,128]{2,1,0:T(8,128)S(1)}, u32[]{:S(2)}, u32[]{:S(2)}) collective-permute-start(f32[2,32,128]{2,1,0:T(8,128)S(1)} %slice_bitcast_fusion.45), channel_id=1, source_target_pairs={{4,0},{8,4},{12,8},{16,12},{20,16},{24,20},{28,24},{32,28},{36,32}... | collective-permute-start | bytes 98312 | tf_op jit(solution)/shard_map/ppermute | solution.py:12
  155.0 6.0 %collective-permute-start.19 = (f32[2,2,32,128]{3,2,1,0:T(8,128)S(1)}, f32[2,2,32,128]{3,2,1,0:T(8,128)S(1)}, u32[]{:S(2)}, u32[]{:S(2)}) collective-permute-start(f32[2,2,32,128]{3,2,1,0:T(8,128)S(1)} %pad_maximum_fusion.13), channel_id=1, source_target_pairs={{4,0},{8,4},{12,8},{16,12},{20,16},{24,20},{28,24},{32,28},{36,32}... | collective-permute-start | bytes 196616 | tf_op jit(solution)/shard_map/ppermute | solution.py:12
  166.3 95.4 %all-to-all-start.1 = ((f32[4,1,32768]{2,1,0:T(1,128)}), f32[4,1,32768]{2,1,0:T(1,128)S(1)}, u32[]{:S(2)}, u32[]{:S(2)}) async-start(f32[4,1,32768]{2,1,0:T(1,128)} %broadcast_in_dim.71), calls=%async_computation.1 | async-start | bytes 1048576 | tf_op jit(solution)/shard_map/all_to_all | solution.py:17
  172.4 16.9 %collective-permute-start.20 = (f32[2,2,32,128]{3,2,1,0:T(8,128)S(1)}, f32[2,2,32,128]{3,2,1,0:T(8,128)S(1)}, u32[]{:S(2)}, u32[]{:S(2)}) collective-permute-start(f32[2,2,32,128]{3,2,1,0:T(8,128)S(1)} %pad_maximum_fusion.14), channel_id=1, source_target_pairs={{0,4},{4,8},{8,12},{12,16},{16,20},{20,24},{24,28},{28,32},{32,36}... | collective-permute-start | bytes 196616 | tf_op jit(solution)/shard_map/ppermute | solution.py:12
  176.7 7.2 %collective-permute-start.21 = (f32[2,32,128]{2,1,0:T(8,128)S(1)}, f32[2,32,128]{2,1,0:T(8,128)S(1)}, u32[]{:S(2)}, u32[]{:S(2)}) collective-permute-start(f32[2,32,128]{2,1,0:T(8,128)S(1)} %slice_bitcast_fusion.35), channel_id=1, source_target_pairs={{4,0},{8,4},{12,8},{16,12},{20,16},{24,20},{28,24},{32,28},{36,32}... | collective-permute-start | bytes 98312 | tf_op jit(solution)/shard_map/ppermute | solution.py:12
  189.6 6.0 %collective-permute-start.23 = (f32[2,2,32,128]{3,2,1,0:T(8,128)S(1)}, f32[2,2,32,128]{3,2,1,0:T(8,128)S(1)}, u32[]{:S(2)}, u32[]{:S(2)}) collective-permute-start(f32[2,2,32,128]{3,2,1,0:T(8,128)S(1)} %pad_maximum_fusion.15), channel_id=1, source_target_pairs={{4,0},{8,4},{12,8},{16,12},{20,16},{24,20},{28,24},{32,28},{36,32}... | collective-permute-start | bytes 196616 | tf_op jit(solution)/shard_map/ppermute | solution.py:12
  201.0 11.7 %collective-permute-start.24 = (f32[2,2,32,128]{3,2,1,0:T(8,128)S(1)}, f32[2,2,32,128]{3,2,1,0:T(8,128)S(1)}, u32[]{:S(2)}, u32[]{:S(2)}) collective-permute-start(f32[2,2,32,128]{3,2,1,0:T(8,128)S(1)} %pad_maximum_fusion.16), channel_id=1, source_target_pairs={{0,4},{4,8},{8,12},{12,16},{16,20},{20,24},{24,28},{28,32},{32,36}... | collective-permute-start | bytes 196616 | tf_op jit(solution)/shard_map/ppermute | solution.py:12
  205.3 7.3 %collective-permute-start.25 = (f32[2,32,128]{2,1,0:T(8,128)S(1)}, f32[2,32,128]{2,1,0:T(8,128)S(1)}, u32[]{:S(2)}, u32[]{:S(2)}) collective-permute-start(f32[2,32,128]{2,1,0:T(8,128)S(1)} %slice_bitcast_fusion.25), channel_id=1, source_target_pairs={{4,0},{8,4},{12,8},{16,12},{20,16},{24,20},{28,24},{32,28},{36,32}... | collective-permute-start | bytes 98312 | tf_op jit(solution)/shard_map/ppermute | solution.py:12
  218.3 6.8 %collective-permute-start.26 = (f32[2,32,128]{2,1,0:T(8,128)S(1)}, f32[2,32,128]{2,1,0:T(8,128)S(1)}, u32[]{:S(2)}, u32[]{:S(2)}) collective-permute-start(f32[2,32,128]{2,1,0:T(8,128)S(1)} %slice_bitcast_fusion.24), channel_id=1, source_target_pairs={{0,4},{4,8},{8,12},{12,16},{16,20},{20,24},{24,28},{28,32},{32,36}... | collective-permute-start | bytes 98312 | tf_op jit(solution)/shard_map/ppermute | solution.py:12
  222.9 7.5 %collective-permute-start.27 = (f32[2,2,32,128]{3,2,1,0:T(8,128)}, f32[2,2,32,128]{3,2,1,0:T(8,128)}, u32[]{:S(2)}, u32[]{:S(2)}) collective-permute-start(f32[2,2,32,128]{3,2,1,0:T(8,128)} %pad_maximum_fusion.17), channel_id=1, source_target_pairs={{4,0},{8,4},{12,8},{16,12},{20,16},{24,20},{28,24},{32,28},{36,32}... | collective-permute-start | bytes 196616 | tf_op jit(solution)/shard_map/ppermute | solution.py:12
  228.5 13.1 %collective-permute-start.29 = (f32[2,32,128]{2,1,0:T(8,128)}, f32[2,32,128]{2,1,0:T(8,128)S(1)}, u32[]{:S(2)}, u32[]{:S(2)}) collective-permute-start(f32[2,32,128]{2,1,0:T(8,128)} %slice_bitcast_fusion.15), channel_id=1, source_target_pairs={{4,0},{8,4},{12,8},{16,12},{20,16},{24,20},{28,24},{32,28},{36,32}... | collective-permute-start | bytes 98312 | tf_op jit(solution)/shard_map/ppermute | solution.py:12
  232.4 9.1 %collective-permute-start.28 = (f32[2,2,32,128]{3,2,1,0:T(8,128)S(1)}, f32[2,2,32,128]{3,2,1,0:T(8,128)S(1)}, u32[]{:S(2)}, u32[]{:S(2)}) collective-permute-start(f32[2,2,32,128]{3,2,1,0:T(8,128)S(1)} %pad_maximum_fusion.18), channel_id=1, source_target_pairs={{0,4},{4,8},{8,12},{12,16},{16,20},{20,24},{24,28},{28,32},{32,36}... | collective-permute-start | bytes 196616 | tf_op jit(solution)/shard_map/ppermute | solution.py:12
  250.0 10.2 %collective-permute-start.31 = (f32[2,2,32,128]{3,2,1,0:T(8,128)S(1)}, f32[2,2,32,128]{3,2,1,0:T(8,128)S(1)}, u32[]{:S(2)}, u32[]{:S(2)}) collective-permute-start(f32[2,2,32,128]{3,2,1,0:T(8,128)S(1)} %pad_maximum_fusion.19), channel_id=1, source_target_pairs={{4,0},{8,4},{12,8},{16,12},{20,16},{24,20},{28,24},{32,28},{36,32}... | collective-permute-start | bytes 196616 | tf_op jit(solution)/shard_map/ppermute | solution.py:12
  262.8 14.3 %all-to-all-start = ((f32[4,1,32768]{2,1,0:T(1,128)}), f32[4,1,32768]{2,1,0:T(1,128)S(1)}, u32[]{:S(2)}, u32[]{:S(2)}) async-start(f32[4,1,32768]{2,1,0:T(1,128)} %broadcast_in_dim.70), calls=%async_computation | async-start | bytes 1048576 | tf_op jit(solution)/shard_map/all_to_all | solution.py:17
  (41 other events, 299.5 us)
where the time goes:
time: 283 us; the launch traced here: 278 us
  starting transfers between devices  116 us (41%)
  other arithmetic  74.2 us (26%)
  between operations  53 us (19%)
  waiting for transfers between devices  18.3 us (6%)
  local copies, waits for them, and re-layouts  17.2 us (6%)
    ppermute x32, starting transfers between devices, shifted(): lax.ppermute(value, axis, [(source, source + steps) for source in range(f...  108 us
    scatter-add x8, other arithmetic, add_points(): field_in.at[wave_index, place_at, row_index, col_index]  42.5 us
    add x18, other arithmetic, add_points(): field_in.at[wave_index, place_at, row_index, col_index]  11.6 us
    all_to_all x2, waiting for transfers between devices, copy_for_each(): lax.all_to_all(jnp.broadcast_to(value[None], (size, *value.shape)), axis,...  9.44 us
    ppermute x32, waiting for transfers between devices, shifted(): lax.ppermute(value, axis, [(source, source + steps) for source in range(f...  8.83 us
    all_to_all x2, starting transfers between devices, copy_for_each(): lax.all_to_all(jnp.broadcast_to(value[None], (size, *value.shape)), axis,...  7.96 us
  transfers between devices with their start and end apart: 34, of which 9 were waited for; matrix products, arithmetic and copies ran while one was open for 28% of the time, Pallas kernels for 0%

commit v1 on v0

v1 whole, which is shorter than its diff:
```python
import functools

import jax
import jax.numpy as jnp
from jax import lax
from jax.experimental import pallas as pl
from jax.experimental.pallas import tpu as pltpu
from jax.sharding import PartitionSpec as P


time_step = 0.15
VX, VY, VZ, XX, YY, ZZ, XY, XZ, YZ = range(9)
PAD = 3
TOP = 8


def cyclic(value, axis, steps):
    count = lax.axis_size(axis)
    return lax.ppermute(value, axis, [(s, (s + steps) % count) for s in range(count)])


class Fields:
    def __init__(self, ref, wave, rows):
        self.ref, self.wave, self.rows = ref, wave, rows

    def at(self, field, plane, move=0):
        return self.ref[self.wave, field, plane + PAD, TOP + move : TOP + move + self.rows, :]

    def put(self, field, plane, value):
        self.ref[self.wave, field, plane + PAD, TOP : TOP + self.rows, :] = value


def clear(ref, rows, slab, beyond):
    for wave in range(2):
        for field in range(9):
            for plane in range(slab + 2 * PAD):
                inside = PAD <= plane < PAD + slab
                if not (inside or beyond):
                    continue
                zero = jnp.zeros((8, ref.shape[-1]), jnp.float32)
                ref[wave, field, plane, 0:TOP, :] = zero
                ref[wave, field, plane, TOP + rows : TOP + rows + 8, :] = zero
                if not inside:
                    ref[wave, field, plane, TOP : TOP + rows, :] = jnp.zeros(
                        (rows, ref.shape[-1]), jnp.float32
                    )


def y_next(value):
    count = value.shape[1]
    lane = lax.broadcasted_iota(jnp.int32, value.shape, 1)
    return jnp.where(lane == count - 1, 0.0, pltpu.roll(value, count - 1, 1))


def y_last(value):
    lane = lax.broadcasted_iota(jnp.int32, value.shape, 1)
    return jnp.where(lane == 0, 0.0, pltpu.roll(value, 1, 1))


def minus(a, b):
    return a if b is None else a - b


def from_high(b, a):
    return -a if b is None else b - a


def velocity(old, new, plane, scaled, parts, low_xz, low_yz, high_zz, added=None):
    if "x" in parts:
        xx, xy, xz = old.at(XX, plane), old.at(XY, plane), old.at(XZ, plane)
        change = (old.at(XX, plane, 1) - xx) + (xy - y_last(xy)) + minus(xz, low_xz)
        new.put(VX, plane, old.at(VX, plane) + scaled * change)
    if "y" in parts:
        xy, yy, yz = old.at(XY, plane), old.at(YY, plane), old.at(YZ, plane)
        change = (xy - old.at(XY, plane, -1)) + (y_next(yy) - yy) + minus(yz, low_yz)
        new.put(VY, plane, old.at(VY, plane) + scaled * change)
    if "z" in parts:
        xz, yz, zz = old.at(XZ, plane), old.at(YZ, plane), old.at(ZZ, plane)
        change = (xz - old.at(XZ, plane, -1)) + (yz - y_last(yz)) + from_high(high_zz, zz)
        result = old.at(VZ, plane) + scaled * change
        new.put(VZ, plane, result if added is None else result + added)


def stress(old, new, plane, lam, mu, low_vz, high_vx, high_vy, added=None, turn=False):
    vx, vy, vz = new.at(VX, plane), new.at(VY, plane), new.at(VZ, plane)
    e_x = vx - new.at(VX, plane, -1)
    e_y = vy - y_last(vy)
    e_z = minus(vz, low_vz)
    shared = lam * (e_x + e_y + e_z)
    if added is not None:
        shared = shared + added
    twice = 2.0 * mu
    xx = old.at(XX, plane) + (shared + twice * e_x)
    yy = old.at(YY, plane) + (shared + twice * e_y)
    zz = old.at(ZZ, plane) + (shared + twice * e_z)
    new.put(XX, plane, xx)
    new.put(YY, plane, yy)
    new.put(ZZ, plane, zz)
    vx_up, vy_up = from_high(high_vx, vx), from_high(high_vy, vy)
    vz_x, vy_x = new.at(VZ, plane, 1) - vz, new.at(VY, plane, 1) - vy
    vz_y, vx_y = y_next(vz) - vz, y_next(vx) - vx
    new.put(XY, plane, old.at(XY, plane) + mu * (vx_y + vy_x))
    new.put(XZ, plane, old.at(XZ, plane) + mu * (vx_up + vz_x))
    new.put(YZ, plane, old.at(YZ, plane) + mu * (vy_up + vz_y))
    total = xx + yy + zz
    if not turn:
        return total, None
    return total, (vz_y - vy_up) + (vx_up - vz_x) + (vy_x - vx_y)


def run_alone(first, held, earth, inject, spot, amount, above, below, rows, slab, span, start):
    for level in range(span):
        left = span - 1 - level
        for wave in range(2):
            old = Fields(first if level == 0 else held, wave, rows)
            new = Fields(held, wave, rows)
            for name, field in enumerate((XZ, YZ)):
                above[level, name, wave] = old.at(field, slab - 1)
            below[level, 0, wave] = old.at(ZZ, 0)
            for plane in range(slab):
                near_low, near_high = plane - left, slab - 1 - plane - left
                parts = "".join(
                    part
                    for part in "xyz"
                    if near_low <= (0 if part != "z" else -1)
                    or near_high <= (0 if part == "z" else -1)
                    or left == span - 1
                )
                velocity(
                    old,
                    new,
                    plane,
                    time_step * earth[0, plane],
                    parts if left < 2 else "xyz",
                    old.at(XZ, plane - 1) if plane else None,
                    old.at(YZ, plane - 1) if plane else None,
                    old.at(ZZ, plane + 1) if plane < slab - 1 else None,
                    inject[start + level, plane] if wave == 1 else None,
                )
            above[level, 2, wave] = new.at(VZ, slab - 1)
            below[level, 1, wave] = new.at(VX, 0)
            below[level, 2, wave] = new.at(VY, 0)
            if left == 0:
                continue
            for plane in range(slab):
                if left == 1 and 0 < plane < slab - 1:
                    continue
                stress(
                    old,
                    new,
                    plane,
                    time_step * earth[1, plane],
                    time_step * earth[2, plane],
                    new.at(VZ, plane - 1) if plane else None,
                    new.at(VX, plane + 1) if plane < slab - 1 else None,
                    new.at(VY, plane + 1) if plane < slab - 1 else None,
                    spot[...] * amount(level, plane) if wave == 0 else None,
                )


def run_true(held, earth, low_earth, high_earth, inject, spot, amount, low, high, image,
             keep_low, keep_high, rows, slab, span, start):
    def from_below(level, name, wave):
        return jnp.where(keep_low, low[level, name, wave], 0.0)

    def from_above(level, name, wave):
        return jnp.where(keep_high, high[level, name, wave], 0.0)

    def medium(kind, plane):
        if plane < 0:
            value = jnp.where(keep_low, low_earth[kind, plane + low_earth.shape[1]], 0.0)
        elif plane >= slab:
            value = jnp.where(keep_high, high_earth[kind, plane - slab], 0.0)
        else:
            value = earth[kind, plane]
        return time_step * value

    for level in range(span):
        done, left = level + 1, span - 1 - level
        moving = {}
        for plane in range(slab):
            moving[plane] = "xyz"
        for far in range(1, PAD):
            if done >= far and left >= far - 1:
                first, last = done == far, left == far - 1
                moving[-far] = "z" if first or last else "xyz"
                moving[slab - 1 + far] = "xy" if first or last else "xyz"
        for wave in range(2):
            both = Fields(held, wave, rows)
            for plane, parts in sorted(moving.items()):
                low_xz, low_yz = both.at(XZ, plane - 1), both.at(YZ, plane - 1)
                high_zz = both.at(ZZ, plane + 1)
                if plane == 0:
                    low_xz = low_xz + from_below(level, 0, wave)
                    low_yz = low_yz + from_below(level, 1, wave)
                if plane == slab - 1:
                    high_zz = high_zz + from_above(level, 0, wave)
                own = 0 <= plane < slab
                velocity(
                    both,
                    both,
                    plane,
                    medium(0, plane),
                    parts,
                    low_xz,
                    low_yz,
                    high_zz,
                    inject[start + level, plane] if own and wave == 1 else None,
                )
        shaking = list(range(slab))
        for far in range(1, PAD):
            if done >= far and left >= far:
                shaking += [-far, slab - 1 + far]
        for plane in sorted(shaking):
            own = 0 <= plane < slab
            found = []
            for wave in range(2):
                both = Fields(held, wave, rows)
                low_vz = both.at(VZ, plane - 1)
                high_vx, high_vy = both.at(VX, plane + 1), both.at(VY, plane + 1)
                if plane == 0:
                    low_vz = low_vz + from_below(level, 2, wave)
                if plane == slab - 1:
                    high_vx = high_vx + from_above(level, 1, wave)
                    high_vy = high_vy + from_above(level, 2, wave)
                found.append(
                    stress(
                        both,
                        both,
                        plane,
                        medium(1, plane),
                        medium(2, plane),
                        low_vz,
                        high_vx,
                        high_vy,
                        spot[...] * amount(level, plane) if own and wave == 0 else None,
                        turn=own and wave == 1,
                    )
                )
            if own:
                (source, _), (receiver, rotation) = found
                image[0, plane] += source * receiver
                image[1, plane] += source * rotation


def set_up(numbers, wavelet, spot, start):
    shape = spot.shape
    row = lax.broadcasted_iota(jnp.int32, shape, 0)
    column = lax.broadcasted_iota(jnp.int32, shape, 1)
    hit = (row == numbers[1]) & (column == numbers[2])
    spot[...] = jnp.where(hit, time_step, 0.0)

    def amount(level, plane):
        return jnp.where(numbers[0] == plane, wavelet[start + level], 0.0)

    return amount


def first_kernel(sizes, wavefields, earth, numbers, wavelet, rows_of, columns_of, traces,
                 above, below, inject, first, held, spot, arrived):
    rows, slab, span, steps = sizes
    fetch = pltpu.make_async_copy(
        wavefields.at[0], first.at[:, :, PAD : PAD + slab, TOP : TOP + rows, :], arrived
    )
    fetch.start()
    width = spot.shape[1]
    receivers = rows_of.shape[1]
    which = lax.broadcasted_iota(jnp.int32, (slab * rows, receivers), 0) == rows_of[...]
    which = which.astype(jnp.float32)
    where = lax.broadcasted_iota(jnp.int32, (receivers, width), 1) == columns_of[...]
    for step in range(steps):
        table = jnp.where(where, time_step * traces[:, step : step + 1], 0.0)
        dense = jnp.dot(
            which, table, precision=lax.Precision.HIGHEST, preferred_element_type=jnp.float32
        )
        inject[step] = dense.reshape(slab, rows, width)
    clear(first, rows, slab, False)
    clear(held, rows, slab, False)
    amount = set_up(numbers, wavelet, spot, 0)
    fetch.wait()
    run_alone(first, held, earth, inject, spot, amount, above, below, rows, slab, span, 0)


def middle_kernel(sizes, wavefields, earth, low_earth, high_earth, numbers, wavelet, inject,
                  low, high, fields, image, above, below, first, held, spot, arrived):
    rows, slab, span, steps = sizes
    inside = first.at[:, :, PAD : PAD + slab, TOP : TOP + rows, :]
    fetch = pltpu.make_async_copy(wavefields.at[0], inside, arrived)
    fetch.start()
    clear(first, rows, slab, True)
    clear(held, rows, slab, False)
    amount = set_up(numbers, wavelet, spot, 0)
    later = set_up(numbers, wavelet, spot, span)
    image[...] = jnp.zeros_like(image)
    fetch.wait()
    run_true(first, earth, low_earth, high_earth, inject, spot, amount, low, high, image,
             numbers[3] > 0, numbers[4] > 0, rows, slab, span, 0)
    store = pltpu.make_async_copy(inside, fields, arrived)
    store.start()
    run_alone(first, held, earth, inject, spot, later, above, below, rows, slab, span, span)
    store.wait()


def last_kernel(sizes, fields, so_far, earth, low_earth, high_earth, numbers, wavelet, inject,
                low, high, image, first, spot, arrived):
    rows, slab, span, steps = sizes
    fetch = pltpu.make_async_copy(
        fields, first.at[:, :, PAD : PAD + slab, TOP : TOP + rows, :], arrived
    )
    fetch.start()
    clear(first, rows, slab, True)
    amount = set_up(numbers, wavelet, spot, span)
    image[...] = so_far[...]
    fetch.wait()
    run_true(first, earth, low_earth, high_earth, inject, spot, amount, low, high, image,
             numbers[3] > 0, numbers[4] > 0, rows, slab, span, span)


def on_device(
    wavefields,
    earth_model,
    source_depth,
    source_column,
    wavelet,
    receiver_depth,
    receiver_column,
    traces,
):
    _, waves, _, slab, rows, width = wavefields.shape
    steps = wavelet.shape[1]
    span = slab
    assert steps == 2 * span
    sizes = (rows, slab, span, steps)
    position = lax.axis_index("gz")
    offset = position * slab
    numbers = jnp.stack(
        [
            source_depth[0] - offset,
            source_column[0] // width,
            source_column[0] % width,
            position,
            lax.axis_size("gz") - 1 - position,
        ]
    ).astype(jnp.int32)
    rows_of = (receiver_depth - offset) * rows + receiver_column // width
    columns_of = (receiver_column % width).reshape(-1, 1)
    by_receiver = traces[0].T

    low_earth = cyclic(earth_model[:, slab - 2 :], "gz", 1)
    high_earth = cyclic(earth_model[:, :2], "gz", -1)

    vmem = pl.BlockSpec(memory_space=pltpu.VMEM)
    smem = pl.BlockSpec(memory_space=pltpu.SMEM)
    anywhere = pl.BlockSpec(memory_space=pl.ANY)
    held = pltpu.VMEM((waves, 9, slab + 2 * PAD, rows + 16, width), jnp.float32)
    spot = pltpu.VMEM((rows, width), jnp.float32)
    arrived = pltpu.SemaphoreType.DMA
    history = jax.ShapeDtypeStruct((span, 3, waves, rows, width), jnp.float32)
    dense = jax.ShapeDtypeStruct((steps, slab, rows, width), jnp.float32)
    images = jax.ShapeDtypeStruct((2, slab, rows, width), jnp.float32)
    kept = jax.ShapeDtypeStruct(wavefields.shape[1:], jnp.float32)
    work = waves * 9 * slab * rows * width

    def cost(scale):
        return pl.CostEstimate(flops=scale * work, bytes_accessed=4 * work, transcendentals=0)

    above, below, inject = pl.pallas_call(
        functools.partial(first_kernel, sizes),
        out_shape=(history, history, dense),
        in_specs=[anywhere, vmem, smem, smem, vmem, vmem, vmem],
        out_specs=(vmem, vmem, vmem),
        scratch_shapes=[held, held, spot, arrived],
        cost_estimate=cost(40),
        name="first",
    )(wavefields, earth_model, numbers, wavelet[0], rows_of, columns_of, by_receiver)
    low = cyclic(above, "gz", 1)
    high = cyclic(below, "gz", -1)
    fields, image, above, below = pl.pallas_call(
        functools.partial(middle_kernel, sizes),
        out_shape=(kept, images, history, history),
        in_specs=[anywhere, vmem, vmem, vmem, smem, smem, vmem, vmem, vmem],
        out_specs=(anywhere, vmem, vmem, vmem),
        scratch_shapes=[held, held, spot, arrived],
        cost_estimate=cost(100),
        name="middle",
    )(wavefields, earth_model, low_earth, high_earth, numbers, wavelet[0], inject, low, high)
    low = cyclic(above, "gz", 1)
    high = cyclic(below, "gz", -1)
    image = pl.pallas_call(
        functools.partial(last_kernel, sizes),
        out_shape=images,
        in_specs=[anywhere, vmem, vmem, vmem, vmem, smem, smem, vmem, vmem, vmem],
        out_specs=vmem,
        scratch_shapes=[held, spot, arrived],
        cost_estimate=cost(60),
        name="last",
    )(fields, image, earth_model, low_earth, high_earth, numbers, wavelet[0], inject, low, high)

    total = image
    for far in range(1, lax.axis_size("shot")):
        total = total + cyclic(image, "shot", far)
    return total * jnp.array([1.0 / (9 * steps), 1.0 / (3 * steps)], jnp.float32).reshape(2, 1, 1, 1)


def solution(mesh):
    placed = (
        P(("parts", "shot"), None, None, "gz", None, None),
        P("parts", "gz", None, None),
        P(("parts", "shot")),
        P(("parts", "shot")),
        P(("parts", "shot"), None),
        P(("parts", "shot"), None),
        P(("parts", "shot"), None),
        P(("parts", "shot"), None, None),
    )
    return jax.shard_map(
        on_device,
        mesh=mesh,
        in_specs=placed,
        out_specs=P("parts", "gz", None, None),
        check_vma=False,
    )
```

time: 283 us -> 74.5 us (0.26)
  the two profiles are of different devices: /device:TPU:33 before, /device:TPU:40 now
where the time goes in v1:
time: 74.5 us; the launch traced here: 74.1 us
  starting transfers between devices  30.6 us (41%)
  waiting for transfers between devices  18.1 us (24%)
  Pallas kernels  16.5 us (22%)
  local copies, waits for them, and re-layouts  4.53 us (6%)
  other arithmetic  2.85 us (4%)
  between operations  1.44 us (2%)
    ppermute x9, starting transfers between devices, cyclic(): lax.ppermute(value, axis, [(s, (s + steps) % count) for s in range(count)])  30.6 us
    ppermute x9, waiting for transfers between devices, cyclic(): lax.ppermute(value, axis, [(s, (s + steps) % count) for s in range(count)])  18.1 us
    pallas_call x1, Pallas kernels, on_device(): pl.pallas_call(functools.partial(middle_kernel, sizes), out_shape=(kept,...  6.73 us
    pallas_call x1, Pallas kernels, on_device(): pl.pallas_call(functools.partial(last_kernel, sizes), out_shape=images, i...  5.47 us
    pallas_call x1, Pallas kernels, on_device(): pl.pallas_call(functools.partial(first_kernel, sizes), out_shape=(history...  4.32 us
    unnamed x17, local copies, waits for them, and re-layouts  3.2 us
    mul x1, other arithmetic, on_device(): total * jnp.array([1.0 / (9 * steps), 1.0 / (3 * steps)], jnp.float32).re...  1.64 us
  transfers between devices with their start and end apart: 9, of which 6 were waited for; matrix products, arithmetic and copies ran while one was open for 0% of the time, Pallas kernels for 0%

profile of v1, /device:TPU:40, one launch (start us, length us, event | category | flops | bytes accessed | tf_op | source)
XLA Modules:
  0.0 74.1 jit_solution(15821385455723608991)
XLA Ops:
  1.4 1.2 %fusion = (s32[64,1]{0,1:T(1,128)S(1)}, s32[1,64]{1,0:T(1,128)}) fusion(s32[1,64]{1,0:T(1,128)} %param.15, s32[1,64]{1,0:T(1,128)} %param.14, s32[]{:T(128)S(6)} %mul.17), kind=kLoop, calls=%fused_computation.6 | loop fusion | flops 1408 | bytes 1028 | tf_op jit(solution)/shard_map/reshape | solution.py:346
  2.6 0.7 copy.11.columns_of
  3.3 1.4 %copy.10 = f32[1,8,64]{1,2,0:T(8,128)} copy(f32[1,8,64]{2,1,0:T(8,128)} %param.16) | data formatting | bytes 4096 | tf_op args[7]
  4.7 0.6 stack.23.numbers
  5.3 4.3 %first.1 = (f32[4,3,2,32,128]{4,3,2,1,0:T(8,128)}, f32[4,3,2,32,128]{4,3,2,1,0:T(8,128)}, f32[8,4,32,128]{3,2,1,0:T(8,128)}) custom-call(f32[1,2,9,4,32,128]{5,4,3,2,1,0:T(8,128)} %wavefields.3, f32[3,4,32,128]{3,2,1,0:T(8,128)} %earth.5, s32[5]{0:T(128)} %stack.23.numbers, f32[8]{0:T(128)} %bitcast.19, s32[1,64]{1,0:T(1,128)} %get-tuple-element.22.rows_of, ...), custom_call_target="tpu_custom_call" | custom-call | flops 11796480 | bytes 1179648 | tf_op jit(solution)/shard_map/first/pallas_call | solution.py:367
  9.7 21.9 %collective-permute-start.3 = (f32[4,3,2,32,128]{4,3,2,1,0:T(8,128)}, f32[4,3,2,32,128]{4,3,2,1,0:T(8,128)S(1)}, u32[]{:S(2)}, u32[]{:S(2)}) collective-permute-start(f32[4,3,2,32,128]{4,3,2,1,0:T(8,128)} %get-tuple-element.14), channel_id=1, source_target_pairs={{0,124},{4,0},{8,4},{12,8},{16,12},{20,16},{24,20},{28,24},{32,28}... | collective-permute-start | bytes 1179656 | tf_op jit(solution)/shard_map/ppermute | solution.py:19
  31.6 0.7 collective-permute-start.1
  32.3 5.9 %collective-permute-done.1.high_earth = f32[3,2,32,128]{3,2,1,0:T(8,128)S(1)} collective-permute-done((f32[3,2,32,128]{3,2,1,0:T(8,128)S(1)}, f32[3,2,32,128]{3,2,1,0:T(8,128)S(1)}, u32[]{:S(2)}, u32[]{:S(2)}) %collective-permute-start.1) | collective-permute-done | bytes 98336 | tf_op jit(solution)/shard_map/ppermute | solution.py:19
  38.3 0.5 copy-done.1
  38.9 0.2 copy-done.3
  39.1 0.1 copy-done.4
  39.2 6.7 %middle.1 = (f32[2,9,4,32,128]{4,3,2,1,0:T(8,128)}, f32[2,4,32,128]{3,2,1,0:T(8,128)}, f32[4,3,2,32,128]{4,3,2,1,0:T(8,128)}, f32[4,3,2,32,128]{4,3,2,1,0:T(8,128)}) custom-call(f32[1,2,9,4,32,128]{5,4,3,2,1,0:T(8,128)} %wavefields.3, f32[3,4,32,128]{3,2,1,0:T(8,128)} %earth.5, f32[3,2,32,128]{3,2,1,0:T(8,128)} %copy-done.2, f32[3,2,32,128]{3,2,1,0:T(8,128)} %copy-done.1, ...), custom_call_target="tpu_custom_call" | custom-call | flops 29491200 | bytes 1179648 | tf_op jit(solution)/shard_map/middle/pallas_call | solution.py:378
  46.0 3.1 %collective-permute-start.5 = (f32[4,3,2,32,128]{4,3,2,1,0:T(8,128)}, f32[4,3,2,32,128]{4,3,2,1,0:T(8,128)S(1)}, u32[]{:S(2)}, u32[]{:S(2)}) collective-permute-start(f32[4,3,2,32,128]{4,3,2,1,0:T(8,128)} %get-tuple-element.18), channel_id=1, source_target_pairs={{0,124},{4,0},{8,4},{12,8},{16,12},{20,16},{24,20},{28,24},{32,28}... | collective-permute-start | bytes 1179656 | tf_op jit(solution)/shard_map/ppermute | solution.py:19
  49.1 5.6 %collective-permute-done.4.low = f32[4,3,2,32,128]{4,3,2,1,0:T(8,128)S(1)} collective-permute-done((f32[4,3,2,32,128]{4,3,2,1,0:T(8,128)}, f32[4,3,2,32,128]{4,3,2,1,0:T(8,128)S(1)}, u32[]{:S(2)}, u32[]{:S(2)}) %collective-permute-start.4) | collective-permute-done | bytes 393248 | tf_op jit(solution)/shard_map/ppermute | solution.py:19
  54.7 0.8 %copy-done.5 = f32[4,3,2,32,128]{4,3,2,1,0:T(8,128)} copy-done((f32[4,3,2,32,128]{4,3,2,1,0:T(8,128)}, f32[4,3,2,32,128]{4,3,2,1,0:T(8,128)S(1)}, u32[]{:S(2)}) %copy-start.5) | copy-done | bytes 393240
  55.5 0.1 copy-done.6
  55.6 5.5 %last.1 = f32[2,4,32,128]{3,2,1,0:T(8,128)} custom-call(f32[2,9,4,32,128]{4,3,2,1,0:T(8,128)} %get-tuple-element.15.fields, f32[2,4,32,128]{3,2,1,0:T(8,128)} %get-tuple-element.16.so_far, f32[3,4,32,128]{3,2,1,0:T(8,128)} %earth.5, f32[3,2,32,128]{3,2,1,0:T(8,128)} %copy-done.2, f32[3,2,32,128]{3,2,1,0:T(8,128)} %copy-done.1, s32[5]{0:T(128)} %stack.23.numbers, ...), custom_call_target="tpu_custom_call" | custom-call | flops 17694720 | bytes 1179648 | tf_op jit(solution)/shard_map/last/pallas_call | solution.py:389
  61.1 3.3 %collective-permute-start.8 = (f32[2,4,32,128]{3,2,1,0:T(8,128)}, f32[2,4,32,128]{3,2,1,0:T(8,128)S(1)}, u32[]{:S(2)}, u32[]{:S(2)}) collective-permute-start(f32[2,4,32,128]{3,2,1,0:T(8,128)} %last.1), channel_id=1, source_target_pairs={{0,3},{1,0},{2,1},{3,2},{4,7},{5,4},{6,5},{7,6},{8,11},{9,8},{10,9... | collective-permute-start | bytes 393224 | tf_op jit(solution)/shard_map/ppermute | solution.py:19
  64.4 0.5 collective-permute-start.7
  64.9 1.0 %collective-permute-start.6 = (f32[2,4,32,128]{3,2,1,0:T(8,128)}, f32[2,4,32,128]{3,2,1,0:T(8,128)S(1)}, u32[]{:S(2)}, u32[]{:S(2)}) collective-permute-start(f32[2,4,32,128]{3,2,1,0:T(8,128)} %last.1), channel_id=1, source_target_pairs={{0,1},{1,2},{2,3},{3,0},{4,5},{5,6},{6,7},{7,4},{8,9},{9,10},{10,1... | collective-permute-start | bytes 393224 | tf_op jit(solution)/shard_map/ppermute | solution.py:19
  65.9 2.7 %collective-permute-done.8 = f32[2,4,32,128]{3,2,1,0:T(8,128)S(1)} collective-permute-done((f32[2,4,32,128]{3,2,1,0:T(8,128)}, f32[2,4,32,128]{3,2,1,0:T(8,128)S(1)}, u32[]{:S(2)}, u32[]{:S(2)}) %collective-permute-start.8) | collective-permute-done | bytes 131104 | tf_op jit(solution)/shard_map/ppermute | solution.py:19
  68.6 2.5 %collective-permute-done.7 = f32[2,4,32,128]{3,2,1,0:T(8,128)S(1)} collective-permute-done((f32[2,4,32,128]{3,2,1,0:T(8,128)}, f32[2,4,32,128]{3,2,1,0:T(8,128)S(1)}, u32[]{:S(2)}, u32[]{:S(2)}) %collective-permute-start.7) | collective-permute-done | bytes 131104 | tf_op jit(solution)/shard_map/ppermute | solution.py:19
  71.2 1.3 %collective-permute-done.6 = f32[2,4,32,128]{3,2,1,0:T(8,128)S(1)} collective-permute-done((f32[2,4,32,128]{3,2,1,0:T(8,128)}, f32[2,4,32,128]{3,2,1,0:T(8,128)S(1)}, u32[]{:S(2)}, u32[]{:S(2)}) %collective-permute-start.6) | collective-permute-done | bytes 131104 | tf_op jit(solution)/shard_map/ppermute | solution.py:19
  72.5 1.6 %add_multiply_fusion = f32[2,4,32,128]{3,2,1,0:T(8,128)} fusion(f32[2,4,32,128]{3,2,1,0:T(8,128)S(1)} %collective-permute-done.8, f32[2,4,32,128]{3,2,1,0:T(8,128)S(1)} %collective-permute-done.7, f32[2,4,32,128]{3,2,1,0:T(8,128)} %last.1, f32[2,4,32,128]{3,2,1,0:T(8,128)S(1)} %collective-permute-done.6, f32[2]{0:T(128)S(1)} %copy-done.7), kind=kLoop, calls=%fused_computation | loop fusion | flops 131072 | bytes 655368 | tf_op jit(solution)/shard_map/mul | solution.py:402
  (19 shorter events, 0.4 us)
Async XLA Ops:
  0.0 31.6 %copy-start = (f32[3,4,32,128]{3,2,1,0:T(8,128)S(1)}, f32[3,4,32,128]{3,2,1,0:T(8,128)}, u32[]{:S(2)}) copy-start(f32[3,4,32,128]{3,2,1,0:T(8,128)} %earth.5) | copy-start | bytes 589828
  9.6 28.7 %collective-permute-start.2 = (f32[4,3,2,32,128]{4,3,2,1,0:T(8,128)}, f32[4,3,2,32,128]{4,3,2,1,0:T(8,128)S(1)}, u32[]{:S(2)}, u32[]{:S(2)}) collective-permute-start(f32[4,3,2,32,128]{4,3,2,1,0:T(8,128)} %get-tuple-element.13), channel_id=1, source_target_pairs={{0,4},{4,8},{8,12},{12,16},{16,20},{20,24},{24,28},{28,32},{32,36}... | collective-permute-start | bytes 1179656 | tf_op jit(solution)/shard_map/ppermute | solution.py:19
  9.7 28.6 %collective-permute-start.3 = (f32[4,3,2,32,128]{4,3,2,1,0:T(8,128)}, f32[4,3,2,32,128]{4,3,2,1,0:T(8,128)S(1)}, u32[]{:S(2)}, u32[]{:S(2)}) collective-permute-start(f32[4,3,2,32,128]{4,3,2,1,0:T(8,128)} %get-tuple-element.14), channel_id=1, source_target_pairs={{0,124},{4,0},{8,4},{12,8},{16,12},{20,16},{24,20},{28,24},{32,28}... | collective-permute-start | bytes 1179656 | tf_op jit(solution)/shard_map/ppermute | solution.py:19
  31.6 6.5 %collective-permute-start.1 = (f32[3,2,32,128]{3,2,1,0:T(8,128)S(1)}, f32[3,2,32,128]{3,2,1,0:T(8,128)S(1)}, u32[]{:S(2)}, u32[]{:S(2)}) collective-permute-start(f32[3,2,32,128]{3,2,1,0:T(8,128)S(1)} %get-tuple-element.19), channel_id=1, source_target_pairs={{0,124},{4,0},{8,4},{12,8},{16,12},{20,16},{24,20},{28,24},{32,28}... | collective-permute-start | bytes 294920 | tf_op jit(solution)/shard_map/ppermute | solution.py:19
  32.3 6.0 %collective-permute-start = (f32[3,2,32,128]{3,2,1,0:T(8,128)S(1)}, f32[3,2,32,128]{3,2,1,0:T(8,128)S(1)}, u32[]{:S(2)}, u32[]{:S(2)}) collective-permute-start(f32[3,2,32,128]{3,2,1,0:T(8,128)S(1)} %get-tuple-element.20), channel_id=1, source_target_pairs={{0,4},{4,8},{8,12},{12,16},{16,20},{20,24},{24,28},{28,32},{32,36}... | collective-permute-start | bytes 294920 | tf_op jit(solution)/shard_map/ppermute | solution.py:19
  38.2 0.6 copy-start.1
  38.3 0.6 copy-start.2
  38.3 0.8 %copy-start.3 = (f32[4,3,2,32,128]{4,3,2,1,0:T(8,128)}, f32[4,3,2,32,128]{4,3,2,1,0:T(8,128)S(1)}, u32[]{:S(2)}) copy-start(f32[4,3,2,32,128]{4,3,2,1,0:T(8,128)S(1)} %collective-permute-done.2.low) | copy-start | bytes 1179652
  38.3 0.9 %copy-start.4 = (f32[4,3,2,32,128]{4,3,2,1,0:T(8,128)}, f32[4,3,2,32,128]{4,3,2,1,0:T(8,128)S(1)}, u32[]{:S(2)}) copy-start(f32[4,3,2,32,128]{4,3,2,1,0:T(8,128)S(1)} %collective-permute-done.3.high) | copy-start | bytes 1179652
  45.9 8.8 %collective-permute-start.4 = (f32[4,3,2,32,128]{4,3,2,1,0:T(8,128)}, f32[4,3,2,32,128]{4,3,2,1,0:T(8,128)S(1)}, u32[]{:S(2)}, u32[]{:S(2)}) collective-permute-start(f32[4,3,2,32,128]{4,3,2,1,0:T(8,128)} %get-tuple-element.17), channel_id=1, source_target_pairs={{0,4},{4,8},{8,12},{12,16},{16,20},{20,24},{24,28},{28,32},{32,36}... | collective-permute-start | bytes 1179656 | tf_op jit(solution)/shard_map/ppermute | solution.py:19
  46.0 8.7 %collective-permute-start.5 = (f32[4,3,2,32,128]{4,3,2,1,0:T(8,128)}, f32[4,3,2,32,128]{4,3,2,1,0:T(8,128)S(1)}, u32[]{:S(2)}, u32[]{:S(2)}) collective-permute-start(f32[4,3,2,32,128]{4,3,2,1,0:T(8,128)} %get-tuple-element.18), channel_id=1, source_target_pairs={{0,124},{4,0},{8,4},{12,8},{16,12},{20,16},{24,20},{28,24},{32,28}... | collective-permute-start | bytes 1179656 | tf_op jit(solution)/shard_map/ppermute | solution.py:19
  54.7 0.8 %copy-start.5 = (f32[4,3,2,32,128]{4,3,2,1,0:T(8,128)}, f32[4,3,2,32,128]{4,3,2,1,0:T(8,128)S(1)}, u32[]{:S(2)}) copy-start(f32[4,3,2,32,128]{4,3,2,1,0:T(8,128)S(1)} %collective-permute-done.4.low) | copy-start | bytes 1179652
  54.7 0.9 %copy-start.6 = (f32[4,3,2,32,128]{4,3,2,1,0:T(8,128)}, f32[4,3,2,32,128]{4,3,2,1,0:T(8,128)S(1)}, u32[]{:S(2)}) copy-start(f32[4,3,2,32,128]{4,3,2,1,0:T(8,128)S(1)} %collective-permute-done.5.high) | copy-start | bytes 1179652
  55.6 16.8 %copy-start.7 = (f32[2]{0:T(128)S(1)}, f32[2]{0:T(128)}, u32[]{:S(2)}) copy-start(f32[2]{0:T(128)} %constant.57.clone) | copy-start | bytes 28
  61.1 7.5 %collective-permute-start.8 = (f32[2,4,32,128]{3,2,1,0:T(8,128)}, f32[2,4,32,128]{3,2,1,0:T(8,128)S(1)}, u32[]{:S(2)}, u32[]{:S(2)}) collective-permute-start(f32[2,4,32,128]{3,2,1,0:T(8,128)} %last.1), channel_id=1, source_target_pairs={{0,3},{1,0},{2,1},{3,2},{4,7},{5,4},{6,5},{7,6},{8,11},{9,8},{10,9... | collective-permute-start | bytes 393224 | tf_op jit(solution)/shard_map/ppermute | solution.py:19
  64.4 6.8 %collective-permute-start.7 = (f32[2,4,32,128]{3,2,1,0:T(8,128)}, f32[2,4,32,128]{3,2,1,0:T(8,128)S(1)}, u32[]{:S(2)}, u32[]{:S(2)}) collective-permute-start(f32[2,4,32,128]{3,2,1,0:T(8,128)} %last.1), channel_id=1, source_target_pairs={{0,2},{1,3},{2,0},{3,1},{4,6},{5,7},{6,4},{7,5},{8,10},{9,11},{10,... | collective-permute-start | bytes 393224 | tf_op jit(solution)/shard_map/ppermute | solution.py:19
  64.9 7.6 %collective-permute-start.6 = (f32[2,4,32,128]{3,2,1,0:T(8,128)}, f32[2,4,32,128]{3,2,1,0:T(8,128)S(1)}, u32[]{:S(2)}, u32[]{:S(2)}) collective-permute-start(f32[2,4,32,128]{3,2,1,0:T(8,128)} %last.1), channel_id=1, source_target_pairs={{0,1},{1,2},{2,3},{3,0},{4,5},{5,6},{6,7},{7,4},{8,9},{9,10},{10,1... | collective-permute-start | bytes 393224 | tf_op jit(solution)/shard_map/ppermute | solution.py:19

commit v2 on v1

v2 whole, which is shorter than its diff:
```python
import functools

import jax
import jax.numpy as jnp
from jax import lax
from jax.experimental import pallas as pl
from jax.experimental.pallas import tpu as pltpu
from jax.sharding import PartitionSpec as P


time_step = 0.15
VX, VY, VZ, XX, YY, ZZ, XY, XZ, YZ = range(9)
PAD = 3
TOP = 8
LIMIT = 24 * 1024 * 1024


def cyclic(value, axis, steps):
    count = lax.axis_size(axis)
    return lax.ppermute(value, axis, [(s, (s + steps) % count) for s in range(count)])


def swapped(value, axis, first):
    count = lax.axis_size(axis)
    partner = {s: s for s in range(count)}
    for s in range(first, count - 1, 2):
        partner[s], partner[s + 1] = s + 1, s
    return lax.ppermute(value, axis, sorted(partner.items()))


class Fields:
    def __init__(self, ref, wave, rows):
        self.ref, self.wave, self.rows = ref, wave, rows

    def at(self, field, plane, move=0):
        return self.ref[self.wave, field, plane + PAD, TOP + move : TOP + move + self.rows, :]

    def put(self, field, plane, value):
        self.ref[self.wave, field, plane + PAD, TOP : TOP + self.rows, :] = value


def clear_margins(ref, rows, planes):
    zero = jnp.zeros((8, ref.shape[-1]), jnp.float32)
    for wave in range(2):
        for field in range(9):
            for plane in planes:
                ref[wave, field, plane + PAD, 0:TOP, :] = zero
                ref[wave, field, plane + PAD, TOP + rows : TOP + rows + 8, :] = zero


def clear_planes(ref, rows, planes):
    zero = jnp.zeros((rows, ref.shape[-1]), jnp.float32)
    for wave in range(2):
        for field in range(9):
            for plane in planes:
                ref[wave, field, plane + PAD, TOP : TOP + rows, :] = zero


def beyond(slab):
    return [*range(-PAD, 0), *range(slab, slab + PAD)]


def y_next(value):
    count = value.shape[1]
    lane = lax.broadcasted_iota(jnp.int32, value.shape, 1)
    return jnp.where(lane == count - 1, 0.0, pltpu.roll(value, count - 1, 1))


def y_last(value):
    lane = lax.broadcasted_iota(jnp.int32, value.shape, 1)
    return jnp.where(lane == 0, 0.0, pltpu.roll(value, 1, 1))


def minus(a, b):
    return a if b is None else a - b


def from_high(b, a):
    return -a if b is None else b - a


def velocity(old, new, plane, scaled, parts, low_xz, low_yz, high_zz, added=None):
    if "x" in parts:
        xx, xy, xz = old.at(XX, plane), old.at(XY, plane), old.at(XZ, plane)
        change = (old.at(XX, plane, 1) - xx) + (xy - y_last(xy)) + minus(xz, low_xz)
        new.put(VX, plane, old.at(VX, plane) + scaled * change)
    if "y" in parts:
        xy, yy, yz = old.at(XY, plane), old.at(YY, plane), old.at(YZ, plane)
        change = (xy - old.at(XY, plane, -1)) + (y_next(yy) - yy) + minus(yz, low_yz)
        new.put(VY, plane, old.at(VY, plane) + scaled * change)
    if "z" in parts:
        xz, yz, zz = old.at(XZ, plane), old.at(YZ, plane), old.at(ZZ, plane)
        change = (xz - old.at(XZ, plane, -1)) + (yz - y_last(yz)) + from_high(high_zz, zz)
        result = old.at(VZ, plane) + scaled * change
        new.put(VZ, plane, result if added is None else result + added)


def stress(old, new, plane, lam, mu, twice, low_vz, high_vx, high_vy, added=None, turn=False):
    vx, vy, vz = new.at(VX, plane), new.at(VY, plane), new.at(VZ, plane)
    e_x = vx - new.at(VX, plane, -1)
    e_y = vy - y_last(vy)
    e_z = minus(vz, low_vz)
    shared = lam * (e_x + e_y + e_z)
    if added is not None:
        shared = shared + added
    xx = old.at(XX, plane) + (shared + twice * e_x)
    yy = old.at(YY, plane) + (shared + twice * e_y)
    zz = old.at(ZZ, plane) + (shared + twice * e_z)
    new.put(XX, plane, xx)
    new.put(YY, plane, yy)
    new.put(ZZ, plane, zz)
    vx_up, vy_up = from_high(high_vx, vx), from_high(high_vy, vy)
    vz_x, vy_x = new.at(VZ, plane, 1) - vz, new.at(VY, plane, 1) - vy
    vz_y, vx_y = y_next(vz) - vz, y_next(vx) - vx
    new.put(XY, plane, old.at(XY, plane) + mu * (vx_y + vy_x))
    new.put(XZ, plane, old.at(XZ, plane) + mu * (vx_up + vz_x))
    new.put(YZ, plane, old.at(YZ, plane) + mu * (vy_up + vz_y))
    total = xx + yy + zz
    if not turn:
        return total, None
    return total, (vz_y - vy_up) + (vx_up - vz_x) + (vy_x - vx_y)


def slot(level, name, wave):
    return (level * 3 + name) * 2 + wave


def run_alone(first, held, medium, inject, source, even, chip, cross, rows, slab, span, start):
    for level in range(span):
        left = span - 1 - level
        for wave in range(2):
            old = Fields(first if level == 0 else held, wave, rows)
            new = Fields(held, wave, rows)
            for plane in range(slab):
                near_low, near_high = plane - left, slab - 1 - plane - left
                parts = "xyz"
                if left < 2:
                    parts = "".join(
                        part
                        for part in "xyz"
                        if near_low <= (-1 if part == "z" else 0)
                        or near_high <= (0 if part == "z" else -1)
                    )
                velocity(
                    old,
                    new,
                    plane,
                    medium[0, plane],
                    parts,
                    old.at(XZ, plane - 1) if plane else None,
                    old.at(YZ, plane - 1) if plane else None,
                    old.at(ZZ, plane + 1) if plane < slab - 1 else None,
                    inject[start + level, plane] if wave == 1 else None,
                )
            top = slab - 1
            above = (old.at(XZ, top), new.at(VZ, top), old.at(YZ, top))
            below = (old.at(ZZ, 0), new.at(VX, 0), new.at(VY, 0))
            for name in range(3):
                chip[slot(level, name, wave)] = jnp.where(even, above[name], below[name])
                cross[slot(level, name, wave)] = jnp.where(even, below[name], above[name])
            if left == 0:
                continue
            for plane in range(slab):
                if left == 1 and 0 < plane < slab - 1:
                    continue
                stress(
                    old,
                    new,
                    plane,
                    medium[1, plane],
                    medium[2, plane],
                    medium[3, plane],
                    new.at(VZ, plane - 1) if plane else None,
                    new.at(VX, plane + 1) if plane < slab - 1 else None,
                    new.at(VY, plane + 1) if plane < slab - 1 else None,
                    source[start + level, plane] if wave == 0 else None,
                )


def run_true(held, medium, halo, inject, source, flags, chip, cross, image, fresh,
             rows, slab, span, start):
    even, keep_low, keep_high = flags

    def from_below(level, name, wave):
        at = slot(level, name, wave)
        return jnp.where(keep_low, jnp.where(even, cross[at], chip[at]), 0.0)

    def from_above(level, name, wave):
        at = slot(level, name, wave)
        return jnp.where(keep_high, jnp.where(even, chip[at], cross[at]), 0.0)

    def around(kind, plane):
        if plane < 0:
            return halo[0, kind, plane + 2]
        if plane >= slab:
            return halo[1, kind, plane - slab]
        return medium[kind, plane]

    for level in range(span):
        done, left = level + 1, span - 1 - level
        moving = {plane: "xyz" for plane in range(slab)}
        for far in range(1, PAD):
            if done >= far and left >= far - 1:
                edge = done == far or left == far - 1
                moving[-far] = "z" if edge else "xyz"
                moving[slab - 1 + far] = "xy" if edge else "xyz"
        for wave in range(2):
            both = Fields(held, wave, rows)
            for plane, parts in sorted(moving.items()):
                low_xz, low_yz = both.at(XZ, plane - 1), both.at(YZ, plane - 1)
                high_zz = both.at(ZZ, plane + 1)
                if plane == 0:
                    low_xz = low_xz + from_below(level, 0, wave)
                    low_yz = low_yz + from_below(level, 2, wave)
                if plane == slab - 1:
                    high_zz = high_zz + from_above(level, 0, wave)
                own = 0 <= plane < slab
                velocity(
                    both,
                    both,
                    plane,
                    around(0, plane),
                    parts,
                    low_xz,
                    low_yz,
                    high_zz,
                    inject[start + level, plane] if own and wave == 1 else None,
                )
        shaking = list(range(slab))
        for far in range(1, PAD):
            if done >= far and left >= far:
                shaking += [-far, slab - 1 + far]
        for plane in sorted(shaking):
            own = 0 <= plane < slab
            found = []
            for wave in range(2):
                both = Fields(held, wave, rows)
                low_vz = both.at(VZ, plane - 1)
                high_vx, high_vy = both.at(VX, plane + 1), both.at(VY, plane + 1)
                if plane == 0:
                    low_vz = low_vz + from_below(level, 1, wave)
                if plane == slab - 1:
                    high_vx = high_vx + from_above(level, 1, wave)
                    high_vy = high_vy + from_above(level, 2, wave)
                found.append(
                    stress(
                        both,
                        both,
                        plane,
                        around(1, plane),
                        around(2, plane),
                        around(3, plane),
                        low_vz,
                        high_vx,
                        high_vy,
                        source[start + level, plane] if own and wave == 0 else None,
                        turn=own and wave == 1,
                    )
                )
            if own:
                (given, _), (taken, rotation) = found
                if fresh and level == 0:
                    image[0, plane] = given * taken
                    image[1, plane] = given * rotation
                else:
                    image[0, plane] += given * taken
                    image[1, plane] += given * rotation


def where_am_i():
    position = lax.axis_index("gz")
    return position % 2 == 0, position > 0, position < lax.axis_size("gz") - 1


def dense_points(depth, column, amounts, slab, rows, width, offset, steps, put):
    points = depth.shape[1]
    row = (depth - offset) * rows + column // width
    where = lax.broadcasted_iota(jnp.int32, (width, points), 0) == column % width
    where = where.astype(jnp.bfloat16)
    where = jnp.concatenate([where, where, where], axis=1)
    which = lax.broadcasted_iota(jnp.int32, (slab * rows, points), 0) == row
    for step in range(steps):
        whole = jnp.where(which, time_step * amounts[step : step + 1, :], 0.0)
        high = whole.astype(jnp.bfloat16)
        rest = whole - high.astype(jnp.float32)
        middle = rest.astype(jnp.bfloat16)
        low = (rest - middle.astype(jnp.float32)).astype(jnp.bfloat16)
        planes = lax.dot_general(
            jnp.concatenate([high, middle, low], axis=1),
            where,
            (((1,), (1,)), ((), ())),
            preferred_element_type=jnp.float32,
        )
        put(step, planes.reshape(slab, rows, width))


def first_kernel(sizes, wavefields, earth, *refs):
    rows, width, slab, span, steps = sizes
    scalars, outside, results, inside = refs[:2], refs[2:6], refs[6:12], refs[12:16]
    held, arrived = refs[16:]
    chip, cross, fields, medium, inject, source = results
    source_depth, source_column = scalars
    wavelet, depth, column, traces = inside
    pairs = [*zip(outside, inside), (earth, medium.at[0:3])]
    pairs.append((wavefields.at[0], fields.at[:, :, PAD : PAD + slab, TOP : TOP + rows, :]))
    fetches = [pltpu.make_async_copy(*pair, arrived.at[n]) for n, pair in enumerate(pairs)]
    for fetch in fetches:
        fetch.start()
    clear_margins(fields, rows, range(-PAD, slab + PAD))
    clear_planes(fields, rows, beyond(slab))
    clear_margins(held, rows, range(slab))
    for fetch in fetches[:4]:
        fetch.wait()
    position = lax.axis_index("gz")
    even = position % 2 == 0

    def put(step, planes):
        inject[step] = planes

    dense_points(depth[...], column[...], traces[0], slab, rows, width, position * slab, steps, put)
    row = lax.broadcasted_iota(jnp.int32, (rows, width), 0)
    lane = lax.broadcasted_iota(jnp.int32, (rows, width), 1)
    spot = row * width + lane == source_column[0]
    for plane in range(slab):
        here = source_depth[0] == position * slab + plane
        for step in range(steps):
            amount = jnp.where(here, time_step * wavelet[0, step], 0.0)
            source[step, plane] = jnp.where(spot, amount, 0.0)
    fetches[4].wait()
    for kind in range(3):
        medium[kind] = time_step * medium[kind]
    medium[3] = 2.0 * medium[2]
    for kind in range(3):
        for far in range(2):
            at = slot(span, 0, 0) + kind * 2 + far
            above, below = medium[kind, slab - 2 + far], medium[kind, far]
            chip[at] = jnp.where(even, above, below)
            cross[at] = jnp.where(even, below, above)
    fetches[5].wait()
    run_alone(fields, held, medium, inject, source, even, chip, cross, rows, slab, span, 0)


def middle_kernel(sizes, fields_in, medium, inject, source, chip, cross,
                  fields, halo, image, next_chip, next_cross, held):
    rows, width, slab, span, steps = sizes
    flags = even, keep_low, keep_high = where_am_i()
    for kind in range(3):
        for far in range(2):
            at = slot(span, 0, 0) + kind * 2 + far
            low = jnp.where(keep_low, jnp.where(even, cross[at], chip[at]), 0.0)
            high = jnp.where(keep_high, jnp.where(even, chip[at], cross[at]), 0.0)
            halo[0, kind, far] = low
            halo[1, kind, far] = high
            if kind == 2:
                halo[0, 3, far] = 2.0 * low
                halo[1, 3, far] = 2.0 * high
    clear_margins(held, rows, range(slab))
    run_true(fields, medium, halo, inject, source, flags, chip, cross, image, True,
             rows, slab, span, 0)
    run_alone(fields, held, medium, inject, source, even, next_chip, next_cross,
              rows, slab, span, span)
    clear_planes(fields, rows, beyond(slab))


def last_kernel(sizes, fields_in, medium, halo, inject, source, chip, cross, so_far,
                fields, image):
    rows, width, slab, span, steps = sizes
    image[...] = so_far[...]
    run_true(fields, medium, halo, inject, source, where_am_i(), chip, cross, image, False,
             rows, slab, span, span)


def within(space, *arrays):
    return [pltpu.with_memory_space_constraint(a, space) for a in arrays]


def on_device(
    wavefields,
    earth_model,
    source_depth,
    source_column,
    wavelet,
    receiver_depth,
    receiver_column,
    traces,
):
    _, waves, _, slab, rows, width = wavefields.shape
    steps = wavelet.shape[1]
    span = slab
    assert steps == 2 * span
    sizes = (rows, width, slab, span, steps)

    vmem = pl.BlockSpec(memory_space=pltpu.VMEM)
    smem = pl.BlockSpec(memory_space=pltpu.SMEM)
    anywhere = pl.BlockSpec(memory_space=pl.ANY)

    def room(*shape):
        return pltpu.VMEM(shape, jnp.float32)

    state = room(waves, 9, slab + 2 * PAD, rows + 16, width)
    history = room(slot(span, 0, 0), rows, width)
    with_medium = room(slot(span, 0, 0) + 6, rows, width)
    dense = room(steps, slab, rows, width)
    images = room(2, slab, rows, width)
    work = waves * 9 * slab * rows * width

    def options(scale):
        return dict(
            cost_estimate=pl.CostEstimate(
                flops=scale * work, bytes_accessed=4 * work, transcendentals=0
            ),
            compiler_params=pltpu.CompilerParams(vmem_limit_bytes=LIMIT),
        )

    chip, cross, fields, medium, inject, source = pl.pallas_call(
        functools.partial(first_kernel, sizes),
        out_shape=(with_medium, with_medium, state, room(4, slab, rows, width), dense, dense),
        in_specs=[anywhere, anywhere, smem, smem] + [anywhere] * 4,
        out_specs=(vmem,) * 6,
        scratch_shapes=[
            pltpu.SMEM(wavelet.shape, jnp.float32),
            pltpu.VMEM(receiver_depth.shape, jnp.int32),
            pltpu.VMEM(receiver_column.shape, jnp.int32),
            room(*traces.shape),
            state,
            pltpu.SemaphoreType.DMA((6,)),
        ],
        name="first",
        **options(40),
    )(*within(pltpu.HBM, wavefields, earth_model), source_depth, source_column,
      *within(pltpu.HBM, wavelet, receiver_depth, receiver_column, traces))
    cross = swapped(cross, "gz", 1)
    chip = swapped(chip, "gz", 0)
    fields, halo, image, chip, cross = pl.pallas_call(
        functools.partial(middle_kernel, sizes),
        out_shape=(state, room(2, 4, 2, rows, width), images, history, history),
        in_specs=[vmem] * 6,
        out_specs=(vmem,) * 5,
        scratch_shapes=[state],
        input_output_aliases={0: 0},
        name="middle",
        **options(100),
    )(*within(pltpu.VMEM, fields, medium, inject, source, chip, cross))
    cross = swapped(cross, "gz", 1)
    chip = swapped(chip, "gz", 0)
    _, image = pl.pallas_call(
        functools.partial(last_kernel, sizes),
        out_shape=(state, images),
        in_specs=[vmem] * 8,
        out_specs=(vmem,) * 2,
        input_output_aliases={0: 0},
        name="last",
        **options(60),
    )(*within(pltpu.VMEM, fields, medium, halo, inject, source, chip, cross, image))

    total = image
    for far in range(1, lax.axis_size("shot")):
        total = total + cyclic(image, "shot", far)
    kind = lax.broadcasted_iota(jnp.int32, total.shape, 0)
    return total * jnp.where(kind == 0, 1.0 / (9 * steps), 1.0 / (3 * steps))


def solution(mesh):
    placed = (
        P(("parts", "shot"), None, None, "gz", None, None),
        P("parts", "gz", None, None),
        P(("parts", "shot")),
        P(("parts", "shot")),
        P(("parts", "shot"), None),
        P(("parts", "shot"), None),
        P(("parts", "shot"), None),
        P(("parts", "shot"), None, None),
    )
    return jax.shard_map(
        on_device,
        mesh=mesh,
        in_specs=placed,
        out_specs=P("parts", "gz", None, None),
        check_vma=False,
    )
```

time: 74.5 us -> 57.1 us (0.77)
  the two profiles are of different devices: /device:TPU:40 before, /device:TPU:33 now
where the time goes in v2:
time: 57.1 us; the launch traced here: 57 us
  starting transfers between devices  27.3 us (48%)
  waiting for transfers between devices  20 us (35%)
  Pallas kernels  7.46 us (13%)
  between operations  1.38 us (2%)
  other arithmetic  0.74 us (1%)
    ppermute x4, starting transfers between devices, swapped(): return lax.ppermute(value, axis, sorted(partner.items()))  24.6 us
    ppermute x4, waiting for transfers between devices, swapped(): return lax.ppermute(value, axis, sorted(partner.items()))  15.7 us
    ppermute x3, waiting for transfers between devices, cyclic(): lax.ppermute(value, axis, [(s, (s + steps) % count) for s in range(count)])  4.37 us
    pallas_call x1, Pallas kernels, on_device(): pl.pallas_call(functools.partial(middle_kernel, sizes), out_shape=(state,...  3.02 us
    ppermute x3, starting transfers between devices, cyclic(): lax.ppermute(value, axis, [(s, (s + steps) % count) for s in range(count)])  2.78 us
    pallas_call x1, Pallas kernels, on_device(): pl.pallas_call(functools.partial(first_kernel, sizes), out_shape=(with_me...  2.44 us
    pallas_call x1, Pallas kernels, on_device(): pl.pallas_call(functools.partial(last_kernel, sizes), out_shape=(state, i...  2 us
  transfers between devices with their start and end apart: 7, of which 4 were waited for; matrix products, arithmetic and copies ran while one was open for 0% of the time, Pallas kernels for 0%

profile of v2, /device:TPU:33, one launch (start us, length us, event | category | flops | bytes accessed | tf_op | source)
XLA Modules:
  0.0 57.0 jit_solution(4925727248587402751)
XLA Ops:
  1.3 2.4 %first.1 = (f32[30,32,128]{2,1,0:T(8,128)S(1)}, f32[30,32,128]{2,1,0:T(8,128)S(1)}, f32[2,9,10,48,128]{4,3,2,1,0:T(8,128)S(1)}, f32[4,4,32,128]{3,2,1,0:T(8,128)...) custom-call(f32[1,2,9,4,32,128]{5,4,3,2,1,0:T(8,128)} %wavefields.1, f32[3,4,32,128]{3,2,1,0:T(8,128)} %earth.1, ...), custom_call_target="tpu_custom_call" | custom-call | flops 11796480 | bytes 1179648 | tf_op jit(solution)/shard_map/first/pallas_call | solution.py:415
  3.7 20.5 %collective-permute-start = (f32[30,32,128]{2,1,0:T(8,128)S(1)}, f32[30,32,128]{2,1,0:T(8,128)S(1)}, u32[]{:S(2)}, u32[]{:S(2)}) collective-permute-start(f32[30,32,128]{2,1,0:T(8,128)S(1)} %get-tuple-element.21), channel_id=1, source_target_pairs={{0,4},{4,0},{8,12},{12,8},{16,20},{20,16},{24,28},{28,24},{32,36},... | collective-permute-start | bytes 1474568 | tf_op jit(solution)/shard_map/ppermute | solution.py:28
  24.3 1.9 %collective-permute-start.1 = (f32[30,32,128]{2,1,0:T(8,128)S(1)}, f32[30,32,128]{2,1,0:T(8,128)S(1)}, u32[]{:S(2)}, u32[]{:S(2)}) collective-permute-start(f32[30,32,128]{2,1,0:T(8,128)S(1)} %get-tuple-element.22), channel_id=1, source_target_pairs={{0,0},{4,8},{8,4},{12,16},{16,12},{20,24},{24,20},{28,32},{32,28},... | collective-permute-start | bytes 1474568 | tf_op jit(solution)/shard_map/ppermute | solution.py:28
  26.2 0.0 collective-permute-done.chip
  26.2 8.2 %collective-permute-done.1.cross = f32[30,32,128]{2,1,0:T(8,128)S(1)} collective-permute-done((f32[30,32,128]{2,1,0:T(8,128)S(1)}, f32[30,32,128]{2,1,0:T(8,128)S(1)}, u32[]{:S(2)}, u32[]{:S(2)}) %collective-permute-start.1) | collective-permute-done | bytes 491552 | tf_op jit(solution)/shard_map/ppermute | solution.py:28
  34.4 3.0 %middle.1 = (f32[2,9,10,48,128]{4,3,2,1,0:T(8,128)S(1)}, f32[2,4,2,32,128]{4,3,2,1,0:T(8,128)S(1)}, f32[2,4,32,128]{3,2,1,0:T(8,128)S(1)}, f32[24,32,128]{2,1,0:T(8,128)S(1)}, f32[24,32,128]{2,1,0:T(8,128)S(1)}) custom-call(f32[2,9,10,48,128]{4,3,2,1,0:T(8,128)S(1)} %get-tuple-element.17.fields_in, ...), custom_call_target="tpu_custom_call", output_to_operand_aliasing={{0}: (0, {})} | custom-call | flops 29491200 | bytes 1179648 | tf_op jit(solution)/shard_map/middle/pallas_call | solution.py:434
  37.5 0.1 collective-permute-start.2
  37.6 2.0 %collective-permute-start.3 = (f32[24,32,128]{2,1,0:T(8,128)S(1)}, f32[24,32,128]{2,1,0:T(8,128)S(1)}, u32[]{:S(2)}, u32[]{:S(2)}) collective-permute-start(f32[24,32,128]{2,1,0:T(8,128)S(1)} %get-tuple-element.26), channel_id=1, source_target_pairs={{0,0},{4,8},{8,4},{12,16},{16,12},{20,24},{24,20},{28,32},{32,28},... | collective-permute-start | bytes 1179656 | tf_op jit(solution)/shard_map/ppermute | solution.py:28
  39.6 0.0 collective-permute-done.2.chip
  39.6 7.5 %collective-permute-done.3.cross = f32[24,32,128]{2,1,0:T(8,128)S(1)} collective-permute-done((f32[24,32,128]{2,1,0:T(8,128)S(1)}, f32[24,32,128]{2,1,0:T(8,128)S(1)}, u32[]{:S(2)}, u32[]{:S(2)}) %collective-permute-start.3) | collective-permute-done | bytes 393248 | tf_op jit(solution)/shard_map/ppermute | solution.py:28
  47.0 2.0 %last.1 = (f32[2,9,10,48,128]{4,3,2,1,0:T(8,128)S(1)}, f32[2,4,32,128]{3,2,1,0:T(8,128)S(1)}) custom-call(f32[2,9,10,48,128]{4,3,2,1,0:T(8,128)S(1)} %get-tuple-element.23.fields_in, f32[4,4,32,128]{3,2,1,0:T(8,128)S(1)} %get-tuple-element.18.medium, f32[2,4,2,32,128]{4,3,2,1,0:T(8,128)S(1)} %get-tuple-element.24.halo, ...), custom_call_target="tpu_custom_call", output_to_operand_aliasing={{0}: (0, {})} | custom-call | flops 17694720 | bytes 1179648 | tf_op jit(solution)/shard_map/last/pallas_call | solution.py:446
  49.1 0.1 collective-permute-start.4
  49.2 0.1 collective-permute-start.5
  49.3 2.5 %collective-permute-start.6 = (f32[2,4,32,128]{3,2,1,0:T(8,128)S(1)}, f32[2,4,32,128]{3,2,1,0:T(8,128)S(1)}, u32[]{:S(2)}, u32[]{:S(2)}) collective-permute-start(f32[2,4,32,128]{3,2,1,0:T(8,128)S(1)} %get-tuple-element.28), channel_id=1, source_target_pairs={{0,3},{1,0},{2,1},{3,2},{4,7},{5,4},{6,5},{7,6},{8,11},{9,8},{10,9... | collective-permute-start | bytes 393224 | tf_op jit(solution)/shard_map/ppermute | solution.py:20
  51.9 3.7 %collective-permute-done.4 = f32[2,4,32,128]{3,2,1,0:T(8,128)S(1)} collective-permute-done((f32[2,4,32,128]{3,2,1,0:T(8,128)S(1)}, f32[2,4,32,128]{3,2,1,0:T(8,128)S(1)}, u32[]{:S(2)}, u32[]{:S(2)}) %collective-permute-start.4) | collective-permute-done | bytes 131104 | tf_op jit(solution)/shard_map/ppermute | solution.py:20
  55.6 0.0 collective-permute-done.5
  55.6 0.6 %collective-permute-done.6 = f32[2,4,32,128]{3,2,1,0:T(8,128)S(1)} collective-permute-done((f32[2,4,32,128]{3,2,1,0:T(8,128)S(1)}, f32[2,4,32,128]{3,2,1,0:T(8,128)S(1)}, u32[]{:S(2)}, u32[]{:S(2)}) %collective-permute-start.6) | collective-permute-done | bytes 131104 | tf_op jit(solution)/shard_map/ppermute | solution.py:20
  56.2 0.7 %add_multiply_fusion = f32[2,4,32,128]{3,2,1,0:T(8,128)} fusion(f32[2,4,32,128]{3,2,1,0:T(8,128)S(1)} %collective-permute-done.6, f32[2,4,32,128]{3,2,1,0:T(8,128)S(1)} %collective-permute-done.5, f32[2,4,32,128]{3,2,1,0:T(8,128)S(1)} %get-tuple-element.28, f32[2,4,32,128]{3,2,1,0:T(8,128)S(1)} %collective-permute-done.4, f32[2]{0:T(128)S(1)} %compare_select_fusion), kind=kLoop, calls=%fused_computation | loop fusion | flops 131072 | bytes 655368 | tf_op jit(solution)/shard_map/mul | solution.py:460
  (1 shorter events, 0.0 us)
Async XLA Ops:
  3.7 22.5 %collective-permute-start = (f32[30,32,128]{2,1,0:T(8,128)S(1)}, f32[30,32,128]{2,1,0:T(8,128)S(1)}, u32[]{:S(2)}, u32[]{:S(2)}) collective-permute-start(f32[30,32,128]{2,1,0:T(8,128)S(1)} %get-tuple-element.21), channel_id=1, source_target_pairs={{0,4},{4,0},{8,12},{12,8},{16,20},{20,16},{24,28},{28,24},{32,36},... | collective-permute-start | bytes 1474568 | tf_op jit(solution)/shard_map/ppermute | solution.py:28
  24.3 10.2 %collective-permute-start.1 = (f32[30,32,128]{2,1,0:T(8,128)S(1)}, f32[30,32,128]{2,1,0:T(8,128)S(1)}, u32[]{:S(2)}, u32[]{:S(2)}) collective-permute-start(f32[30,32,128]{2,1,0:T(8,128)S(1)} %get-tuple-element.22), channel_id=1, source_target_pairs={{0,0},{4,8},{8,4},{12,16},{16,12},{20,24},{24,20},{28,32},{32,28},... | collective-permute-start | bytes 1474568 | tf_op jit(solution)/shard_map/ppermute | solution.py:28
  37.5 2.1 %collective-permute-start.2 = (f32[24,32,128]{2,1,0:T(8,128)S(1)}, f32[24,32,128]{2,1,0:T(8,128)S(1)}, u32[]{:S(2)}, u32[]{:S(2)}) collective-permute-start(f32[24,32,128]{2,1,0:T(8,128)S(1)} %get-tuple-element.25), channel_id=1, source_target_pairs={{0,4},{4,0},{8,12},{12,8},{16,20},{20,16},{24,28},{28,24},{32,36},... | collective-permute-start | bytes 1179656 | tf_op jit(solution)/shard_map/ppermute | solution.py:28
  37.6 9.4 %collective-permute-start.3 = (f32[24,32,128]{2,1,0:T(8,128)S(1)}, f32[24,32,128]{2,1,0:T(8,128)S(1)}, u32[]{:S(2)}, u32[]{:S(2)}) collective-permute-start(f32[24,32,128]{2,1,0:T(8,128)S(1)} %get-tuple-element.26), channel_id=1, source_target_pairs={{0,0},{4,8},{8,4},{12,16},{16,12},{20,24},{24,20},{28,32},{32,28},... | collective-permute-start | bytes 1179656 | tf_op jit(solution)/shard_map/ppermute | solution.py:28
  49.1 6.5 %collective-permute-start.4 = (f32[2,4,32,128]{3,2,1,0:T(8,128)S(1)}, f32[2,4,32,128]{3,2,1,0:T(8,128)S(1)}, u32[]{:S(2)}, u32[]{:S(2)}) collective-permute-start(f32[2,4,32,128]{3,2,1,0:T(8,128)S(1)} %get-tuple-element.28), channel_id=1, source_target_pairs={{0,1},{1,2},{2,3},{3,0},{4,5},{5,6},{6,7},{7,4},{8,9},{9,10},{10,1... | collective-permute-start | bytes 393224 | tf_op jit(solution)/shard_map/ppermute | solution.py:20
  49.2 6.4 %collective-permute-start.5 = (f32[2,4,32,128]{3,2,1,0:T(8,128)S(1)}, f32[2,4,32,128]{3,2,1,0:T(8,128)S(1)}, u32[]{:S(2)}, u32[]{:S(2)}) collective-permute-start(f32[2,4,32,128]{3,2,1,0:T(8,128)S(1)} %get-tuple-element.28), channel_id=1, source_target_pairs={{0,2},{1,3},{2,0},{3,1},{4,6},{5,7},{6,4},{7,5},{8,10},{9,11},{10,... | collective-permute-start | bytes 393224 | tf_op jit(solution)/shard_map/ppermute | solution.py:20
  49.3 6.9 %collective-permute-start.6 = (f32[2,4,32,128]{3,2,1,0:T(8,128)S(1)}, f32[2,4,32,128]{3,2,1,0:T(8,128)S(1)}, u32[]{:S(2)}, u32[]{:S(2)}) collective-permute-start(f32[2,4,32,128]{3,2,1,0:T(8,128)S(1)} %get-tuple-element.28), channel_id=1, source_target_pairs={{0,3},{1,0},{2,1},{3,2},{4,7},{5,4},{6,5},{7,6},{8,11},{9,8},{10,9... | collective-permute-start | bytes 393224 | tf_op jit(solution)/shard_map/ppermute | solution.py:20

commit v3 on v2

--- a/solution.py
+++ b/solution.py
@@ -342,7 +342,7 @@
 
 def middle_kernel(sizes, fields_in, medium, inject, source, chip, cross,
                   fields, halo, image, next_chip, next_cross, held):
-    rows, width, slab, span, steps = sizes
+    rows, _, slab, span, _ = sizes
     flags = even, keep_low, keep_high = where_am_i()
     for kind in range(3):
         for far in range(2):
@@ -364,7 +364,7 @@
 
 def last_kernel(sizes, fields_in, medium, halo, inject, source, chip, cross, so_far,
                 fields, image):
-    rows, width, slab, span, steps = sizes
+    rows, _, slab, span, _ = sizes
     image[...] = so_far[...]
     run_true(fields, medium, halo, inject, source, where_am_i(), chip, cross, image, False,
              rows, slab, span, span)
@@ -372,6 +372,12 @@
 
 def within(space, *arrays):
     return [pltpu.with_memory_space_constraint(a, space) for a in arrays]
+
+
+def exchange(chip, cross):
+    cross = swapped(cross, "gz", 1)
+    chip = swapped(chip, "gz", 0)
+    return chip, cross
 
 
 def on_device(
@@ -429,8 +435,7 @@
         **options(40),
     )(*within(pltpu.HBM, wavefields, earth_model), source_depth, source_column,
       *within(pltpu.HBM, wavelet, receiver_depth, receiver_column, traces))
-    cross = swapped(cross, "gz", 1)
-    chip = swapped(chip, "gz", 0)
+    chip, cross = exchange(chip, cross)
     fields, halo, image, chip, cross = pl.pallas_call(
         functools.partial(middle_kernel, sizes),
         out_shape=(state, room(2, 4, 2, rows, width), images, history, history),
@@ -441,8 +446,7 @@
         name="middle",
         **options(100),
     )(*within(pltpu.VMEM, fields, medium, inject, source, chip, cross))
-    cross = swapped(cross, "gz", 1)
-    chip = swapped(chip, "gz", 0)
+    chip, cross = exchange(chip, cross)
     _, image = pl.pallas_call(
         functools.partial(last_kernel, sizes),
         out_shape=(state, images),
@@ -454,7 +458,8 @@
     )(*within(pltpu.VMEM, fields, medium, halo, inject, source, chip, cross, image))
 
     total = image
-    for far in range(1, lax.axis_size("shot")):
+    count = lax.axis_size("shot")
+    for far in sorted(range(1, count), key=lambda far: -min(far, count - far)):
         total = total + cyclic(image, "shot", far)
     kind = lax.broadcasted_iota(jnp.int32, total.shape, 0)
     return total * jnp.where(kind == 0, 1.0 / (9 * steps), 1.0 / (3 * steps))

time: 57.1 us -> 56.6 us (level)
  waiting for transfers between devices: 20 us -> 19.4 us
    ppermute x3, waiting for transfers between devices: 4.37 us -> 3.75 us  [cyclic(): lax.ppermute(value, axis, [(s, (s + steps) % count) for s in range(count)])]
where the time goes in v3:
time: 56.6 us; the launch traced here: 56.5 us
  starting transfers between devices  27.5 us (49%)
  waiting for transfers between devices  19.4 us (34%)
  Pallas kernels  7.46 us (13%)
  between operations  1.38 us (2%)
  other arithmetic  0.74 us (1%)
    ppermute x4, starting transfers between devices, swapped(): return lax.ppermute(value, axis, sorted(partner.items()))  24.6 us
    ppermute x4, waiting for transfers between devices, swapped(): return lax.ppermute(value, axis, sorted(partner.items()))  15.7 us
    ppermute x3, waiting for transfers between devices, cyclic(): lax.ppermute(value, axis, [(s, (s + steps) % count) for s in range(count)])  3.75 us
    pallas_call x1, Pallas kernels, on_device(): pl.pallas_call(functools.partial(middle_kernel, sizes), out_shape=(state,...  3.02 us
    ppermute x3, starting transfers between devices, cyclic(): lax.ppermute(value, axis, [(s, (s + steps) % count) for s in range(count)])  2.92 us
    pallas_call x1, Pallas kernels, on_device(): pl.pallas_call(functools.partial(first_kernel, sizes), out_shape=(with_me...  2.44 us
    pallas_call x1, Pallas kernels, on_device(): pl.pallas_call(functools.partial(last_kernel, sizes), out_shape=(state, i...  2 us
  transfers between devices with their start and end apart: 7, of which 4 were waited for; matrix products, arithmetic and copies ran while one was open for 0% of the time, Pallas kernels for 0%

profile of v3, /device:TPU:33, one launch (start us, length us, event | category | flops | bytes accessed | tf_op | source)
XLA Modules:
  0.0 56.5 jit_solution(16546759440094284406)
XLA Ops:
  1.3 2.4 %first.1 = (f32[30,32,128]{2,1,0:T(8,128)S(1)}, f32[30,32,128]{2,1,0:T(8,128)S(1)}, f32[2,9,10,48,128]{4,3,2,1,0:T(8,128)S(1)}, f32[4,4,32,128]{3,2,1,0:T(8,128)...) custom-call(f32[1,2,9,4,32,128]{5,4,3,2,1,0:T(8,128)} %wavefields.1, f32[3,4,32,128]{3,2,1,0:T(8,128)} %earth.1, ...), custom_call_target="tpu_custom_call" | custom-call | flops 11796480 | bytes 1179648 | tf_op jit(solution)/shard_map/first/pallas_call | solution.py:421
  3.7 20.5 %collective-permute-start = (f32[30,32,128]{2,1,0:T(8,128)S(1)}, f32[30,32,128]{2,1,0:T(8,128)S(1)}, u32[]{:S(2)}, u32[]{:S(2)}) collective-permute-start(f32[30,32,128]{2,1,0:T(8,128)S(1)} %get-tuple-element.21), channel_id=1, source_target_pairs={{0,4},{4,0},{8,12},{12,8},{16,20},{20,16},{24,28},{28,24},{32,36},... | collective-permute-start | bytes 1474568 | tf_op jit(solution)/shard_map/ppermute | solution.py:28
  24.3 1.9 %collective-permute-start.1 = (f32[30,32,128]{2,1,0:T(8,128)S(1)}, f32[30,32,128]{2,1,0:T(8,128)S(1)}, u32[]{:S(2)}, u32[]{:S(2)}) collective-permute-start(f32[30,32,128]{2,1,0:T(8,128)S(1)} %get-tuple-element.22), channel_id=1, source_target_pairs={{0,0},{4,8},{8,4},{12,16},{16,12},{20,24},{24,20},{28,32},{32,28},... | collective-permute-start | bytes 1474568 | tf_op jit(solution)/shard_map/ppermute | solution.py:28
  26.2 0.0 collective-permute-done.chip
  26.2 8.2 %collective-permute-done.1.cross = f32[30,32,128]{2,1,0:T(8,128)S(1)} collective-permute-done((f32[30,32,128]{2,1,0:T(8,128)S(1)}, f32[30,32,128]{2,1,0:T(8,128)S(1)}, u32[]{:S(2)}, u32[]{:S(2)}) %collective-permute-start.1) | collective-permute-done | bytes 491552 | tf_op jit(solution)/shard_map/ppermute | solution.py:28
  34.4 3.0 %middle.1 = (f32[2,9,10,48,128]{4,3,2,1,0:T(8,128)S(1)}, f32[2,4,2,32,128]{4,3,2,1,0:T(8,128)S(1)}, f32[2,4,32,128]{3,2,1,0:T(8,128)S(1)}, f32[24,32,128]{2,1,0:T(8,128)S(1)}, f32[24,32,128]{2,1,0:T(8,128)S(1)}) custom-call(f32[2,9,10,48,128]{4,3,2,1,0:T(8,128)S(1)} %get-tuple-element.17.fields_in, ...), custom_call_target="tpu_custom_call", output_to_operand_aliasing={{0}: (0, {})} | custom-call | flops 29491200 | bytes 1179648 | tf_op jit(solution)/shard_map/middle/pallas_call | solution.py:439
  37.5 0.1 collective-permute-start.2
  37.6 2.0 %collective-permute-start.3 = (f32[24,32,128]{2,1,0:T(8,128)S(1)}, f32[24,32,128]{2,1,0:T(8,128)S(1)}, u32[]{:S(2)}, u32[]{:S(2)}) collective-permute-start(f32[24,32,128]{2,1,0:T(8,128)S(1)} %get-tuple-element.26), channel_id=1, source_target_pairs={{0,0},{4,8},{8,4},{12,16},{16,12},{20,24},{24,20},{28,32},{32,28},... | collective-permute-start | bytes 1179656 | tf_op jit(solution)/shard_map/ppermute | solution.py:28
  39.6 0.0 collective-permute-done.2.chip
  39.6 7.5 %collective-permute-done.3.cross = f32[24,32,128]{2,1,0:T(8,128)S(1)} collective-permute-done((f32[24,32,128]{2,1,0:T(8,128)S(1)}, f32[24,32,128]{2,1,0:T(8,128)S(1)}, u32[]{:S(2)}, u32[]{:S(2)}) %collective-permute-start.3) | collective-permute-done | bytes 393248 | tf_op jit(solution)/shard_map/ppermute | solution.py:28
  47.0 2.0 %last.1 = (f32[2,9,10,48,128]{4,3,2,1,0:T(8,128)S(1)}, f32[2,4,32,128]{3,2,1,0:T(8,128)S(1)}) custom-call(f32[2,9,10,48,128]{4,3,2,1,0:T(8,128)S(1)} %get-tuple-element.23.fields_in, f32[4,4,32,128]{3,2,1,0:T(8,128)S(1)} %get-tuple-element.18.medium, f32[2,4,2,32,128]{4,3,2,1,0:T(8,128)S(1)} %get-tuple-element.24.halo, ...), custom_call_target="tpu_custom_call", output_to_operand_aliasing={{0}: (0, {})} | custom-call | flops 17694720 | bytes 1179648 | tf_op jit(solution)/shard_map/last/pallas_call | solution.py:450
  49.1 0.1 collective-permute-start.4
  49.2 0.1 collective-permute-start.5
  49.3 2.6 %collective-permute-start.6 = (f32[2,4,32,128]{3,2,1,0:T(8,128)S(1)}, f32[2,4,32,128]{3,2,1,0:T(8,128)S(1)}, u32[]{:S(2)}, u32[]{:S(2)}) collective-permute-start(f32[2,4,32,128]{3,2,1,0:T(8,128)S(1)} %get-tuple-element.28), channel_id=1, source_target_pairs={{0,3},{1,0},{2,1},{3,2},{4,7},{5,4},{6,5},{7,6},{8,11},{9,8},{10,9... | collective-permute-start | bytes 393224 | tf_op jit(solution)/shard_map/ppermute | solution.py:20
  52.0 2.6 %collective-permute-done.4 = f32[2,4,32,128]{3,2,1,0:T(8,128)S(1)} collective-permute-done((f32[2,4,32,128]{3,2,1,0:T(8,128)S(1)}, f32[2,4,32,128]{3,2,1,0:T(8,128)S(1)}, u32[]{:S(2)}, u32[]{:S(2)}) %collective-permute-start.4) | collective-permute-done | bytes 131104 | tf_op jit(solution)/shard_map/ppermute | solution.py:20
  54.6 1.1 %collective-permute-done.5 = f32[2,4,32,128]{3,2,1,0:T(8,128)S(1)} collective-permute-done((f32[2,4,32,128]{3,2,1,0:T(8,128)S(1)}, f32[2,4,32,128]{3,2,1,0:T(8,128)S(1)}, u32[]{:S(2)}, u32[]{:S(2)}) %collective-permute-start.5) | collective-permute-done | bytes 131104 | tf_op jit(solution)/shard_map/ppermute | solution.py:20
  55.8 0.0 collective-permute-done.6
  55.8 0.7 %add_multiply_fusion = f32[2,4,32,128]{3,2,1,0:T(8,128)} fusion(f32[2,4,32,128]{3,2,1,0:T(8,128)S(1)} %collective-permute-done.6, f32[2,4,32,128]{3,2,1,0:T(8,128)S(1)} %collective-permute-done.5, f32[2,4,32,128]{3,2,1,0:T(8,128)S(1)} %get-tuple-element.28, f32[2,4,32,128]{3,2,1,0:T(8,128)S(1)} %collective-permute-done.4, f32[2]{0:T(128)S(1)} %compare_select_fusion), kind=kLoop, calls=%fused_computation | loop fusion | flops 131072 | bytes 655368 | tf_op jit(solution)/shard_map/mul | solution.py:465
  (1 shorter events, 0.0 us)
Async XLA Ops:
  3.7 22.5 %collective-permute-start = (f32[30,32,128]{2,1,0:T(8,128)S(1)}, f32[30,32,128]{2,1,0:T(8,128)S(1)}, u32[]{:S(2)}, u32[]{:S(2)}) collective-permute-start(f32[30,32,128]{2,1,0:T(8,128)S(1)} %get-tuple-element.21), channel_id=1, source_target_pairs={{0,4},{4,0},{8,12},{12,8},{16,20},{20,16},{24,28},{28,24},{32,36},... | collective-permute-start | bytes 1474568 | tf_op jit(solution)/shard_map/ppermute | solution.py:28
  24.3 10.2 %collective-permute-start.1 = (f32[30,32,128]{2,1,0:T(8,128)S(1)}, f32[30,32,128]{2,1,0:T(8,128)S(1)}, u32[]{:S(2)}, u32[]{:S(2)}) collective-permute-start(f32[30,32,128]{2,1,0:T(8,128)S(1)} %get-tuple-element.22), channel_id=1, source_target_pairs={{0,0},{4,8},{8,4},{12,16},{16,12},{20,24},{24,20},{28,32},{32,28},... | collective-permute-start | bytes 1474568 | tf_op jit(solution)/shard_map/ppermute | solution.py:28
  37.5 2.1 %collective-permute-start.2 = (f32[24,32,128]{2,1,0:T(8,128)S(1)}, f32[24,32,128]{2,1,0:T(8,128)S(1)}, u32[]{:S(2)}, u32[]{:S(2)}) collective-permute-start(f32[24,32,128]{2,1,0:T(8,128)S(1)} %get-tuple-element.25), channel_id=1, source_target_pairs={{0,4},{4,0},{8,12},{12,8},{16,20},{20,16},{24,28},{28,24},{32,36},... | collective-permute-start | bytes 1179656 | tf_op jit(solution)/shard_map/ppermute | solution.py:28
  37.6 9.4 %collective-permute-start.3 = (f32[24,32,128]{2,1,0:T(8,128)S(1)}, f32[24,32,128]{2,1,0:T(8,128)S(1)}, u32[]{:S(2)}, u32[]{:S(2)}) collective-permute-start(f32[24,32,128]{2,1,0:T(8,128)S(1)} %get-tuple-element.26), channel_id=1, source_target_pairs={{0,0},{4,8},{8,4},{12,16},{16,12},{20,24},{24,20},{28,32},{32,28},... | collective-permute-start | bytes 1179656 | tf_op jit(solution)/shard_map/ppermute | solution.py:28
  49.1 5.5 %collective-permute-start.4 = (f32[2,4,32,128]{3,2,1,0:T(8,128)S(1)}, f32[2,4,32,128]{3,2,1,0:T(8,128)S(1)}, u32[]{:S(2)}, u32[]{:S(2)}) collective-permute-start(f32[2,4,32,128]{3,2,1,0:T(8,128)S(1)} %get-tuple-element.28), channel_id=1, source_target_pairs={{0,2},{1,3},{2,0},{3,1},{4,6},{5,7},{6,4},{7,5},{8,10},{9,11},{10,... | collective-permute-start | bytes 393224 | tf_op jit(solution)/shard_map/ppermute | solution.py:20
  49.2 6.5 %collective-permute-start.5 = (f32[2,4,32,128]{3,2,1,0:T(8,128)S(1)}, f32[2,4,32,128]{3,2,1,0:T(8,128)S(1)}, u32[]{:S(2)}, u32[]{:S(2)}) collective-permute-start(f32[2,4,32,128]{3,2,1,0:T(8,128)S(1)} %get-tuple-element.28), channel_id=1, source_target_pairs={{0,1},{1,2},{2,3},{3,0},{4,5},{5,6},{6,7},{7,4},{8,9},{9,10},{10,1... | collective-permute-start | bytes 393224 | tf_op jit(solution)/shard_map/ppermute | solution.py:20
  49.3 6.4 %collective-permute-start.6 = (f32[2,4,32,128]{3,2,1,0:T(8,128)S(1)}, f32[2,4,32,128]{3,2,1,0:T(8,128)S(1)}, u32[]{:S(2)}, u32[]{:S(2)}) collective-permute-start(f32[2,4,32,128]{3,2,1,0:T(8,128)S(1)} %get-tuple-element.28), channel_id=1, source_target_pairs={{0,3},{1,0},{2,1},{3,2},{4,7},{5,4},{6,5},{7,6},{8,11},{9,8},{10,9... | collective-permute-start | bytes 393224 | tf_op jit(solution)/shard_map/ppermute | solution.py:20

commit v4 on v3

--- a/solution.py
+++ b/solution.py
@@ -95,7 +95,8 @@
         new.put(VZ, plane, result if added is None else result + added)
 
 
-def stress(old, new, plane, lam, mu, twice, low_vz, high_vx, high_vy, added=None, turn=False):
+def stress(old, new, plane, lam, mu, twice, low_vz, high_vx, high_vy, added=None, turn=False,
+           flat=True, keep=True):
     vx, vy, vz = new.at(VX, plane), new.at(VY, plane), new.at(VZ, plane)
     e_x = vx - new.at(VX, plane, -1)
     e_y = vy - y_last(vy)
@@ -103,22 +104,49 @@
     shared = lam * (e_x + e_y + e_z)
     if added is not None:
         shared = shared + added
-    xx = old.at(XX, plane) + (shared + twice * e_x)
-    yy = old.at(YY, plane) + (shared + twice * e_y)
-    zz = old.at(ZZ, plane) + (shared + twice * e_z)
-    new.put(XX, plane, xx)
-    new.put(YY, plane, yy)
-    new.put(ZZ, plane, zz)
-    vx_up, vy_up = from_high(high_vx, vx), from_high(high_vy, vy)
-    vz_x, vy_x = new.at(VZ, plane, 1) - vz, new.at(VY, plane, 1) - vy
-    vz_y, vx_y = y_next(vz) - vz, y_next(vx) - vx
-    new.put(XY, plane, old.at(XY, plane) + mu * (vx_y + vy_x))
-    new.put(XZ, plane, old.at(XZ, plane) + mu * (vx_up + vz_x))
-    new.put(YZ, plane, old.at(YZ, plane) + mu * (vy_up + vz_y))
-    total = xx + yy + zz
-    if not turn:
-        return total, None
-    return total, (vz_y - vy_up) + (vx_up - vz_x) + (vy_x - vx_y)
+    results = [(ZZ, old.at(ZZ, plane) + (shared + twice * e_z))]
+    total = rotation = None
+    if flat:
+        xx = old.at(XX, plane) + (shared + twice * e_x)
+        yy = old.at(YY, plane) + (shared + twice * e_y)
+        total = xx + yy + results[0][1]
+        results += [(XX, xx), (YY, yy)]
+    if keep or turn:
+        vx_up, vy_up = from_high(high_vx, vx), from_high(high_vy, vy)
+        vz_x, vz_y = new.at(VZ, plane, 1) - vz, y_next(vz) - vz
+    if flat and (keep or turn):
+        vy_x, vx_y = new.at(VY, plane, 1) - vy, y_next(vx) - vx
+    if keep:
+        results.append((XZ, old.at(XZ, plane) + mu * (vx_up + vz_x)))
+        results.append((YZ, old.at(YZ, plane) + mu * (vy_up + vz_y)))
+        if flat:
+            results.append((XY, old.at(XY, plane) + mu * (vx_y + vy_x)))
+        for field, result in results:
+            new.put(field, plane, result)
+    if turn:
+        rotation = (vz_y - vy_up) + (vx_up - vz_x) + (vy_x - vx_y)
+    return total, rotation
+
+
+def alone_parts(plane, top, left):
+    near_low, near_high = plane - left, top - plane - left
+    if left >= 2:
+        return "xyz"
+    return "".join(
+        part
+        for part in "xyz"
+        if near_low <= (-1 if part == "z" else 0) or near_high <= (0 if part == "z" else -1)
+    )
+
+
+def true_parts(slab, span, done):
+    moving, left = {plane: "xyz" for plane in range(slab)}, span - done
+    for far in range(1, PAD):
+        if done >= far and left >= far - 1:
+            edge = done == far or left == far - 1
+            moving[-far] = "z" if edge else "xyz"
+            moving[slab - 1 + far] = "xy" if edge else "xyz"
+    return moving
 
 
 def slot(level, name, wave):
@@ -132,15 +160,7 @@
             old = Fields(first if level == 0 else held, wave, rows)
             new = Fields(held, wave, rows)
             for plane in range(slab):
-                near_low, near_high = plane - left, slab - 1 - plane - left
-                parts = "xyz"
-                if left < 2:
-                    parts = "".join(
-                        part
-                        for part in "xyz"
-                        if near_low <= (-1 if part == "z" else 0)
-                        or near_high <= (0 if part == "z" else -1)
-                    )
+                parts = alone_parts(plane, slab - 1, left)
                 velocity(
                     old,
                     new,
@@ -174,11 +194,12 @@
                     new.at(VX, plane + 1) if plane < slab - 1 else None,
                     new.at(VY, plane + 1) if plane < slab - 1 else None,
                     source[start + level, plane] if wave == 0 else None,
+                    flat=alone_parts(plane, slab - 1, left - 1) != "z",
                 )
 
 
 def run_true(held, medium, halo, inject, source, flags, chip, cross, image, fresh,
-             rows, slab, span, start):
+             rows, slab, span, start, final):
     even, keep_low, keep_high = flags
 
     def from_below(level, name, wave):
@@ -198,12 +219,8 @@
 
     for level in range(span):
         done, left = level + 1, span - 1 - level
-        moving = {plane: "xyz" for plane in range(slab)}
-        for far in range(1, PAD):
-            if done >= far and left >= far - 1:
-                edge = done == far or left == far - 1
-                moving[-far] = "z" if edge else "xyz"
-                moving[slab - 1 + far] = "xy" if edge else "xyz"
+        moving = true_parts(slab, span, done)
+        upcoming = true_parts(slab, span, done + 1) if left else moving
         for wave in range(2):
             both = Fields(held, wave, rows)
             for plane, parts in sorted(moving.items()):
@@ -255,6 +272,8 @@
                         high_vy,
                         source[start + level, plane] if own and wave == 0 else None,
                         turn=own and wave == 1,
+                        flat=own or upcoming[plane] != "z",
+                        keep=left > 0 or not final,
                     )
                 )
             if own:
@@ -356,7 +375,7 @@
                 halo[1, 3, far] = 2.0 * high
     clear_margins(held, rows, range(slab))
     run_true(fields, medium, halo, inject, source, flags, chip, cross, image, True,
-             rows, slab, span, 0)
+             rows, slab, span, 0, False)
     run_alone(fields, held, medium, inject, source, even, next_chip, next_cross,
               rows, slab, span, span)
     clear_planes(fields, rows, beyond(slab))
@@ -367,7 +386,7 @@
     rows, _, slab, span, _ = sizes
     image[...] = so_far[...]
     run_true(fields, medium, halo, inject, source, where_am_i(), chip, cross, image, False,
-             rows, slab, span, span)
+             rows, slab, span, span, True)
 
 
 def within(space, *arrays):

time: 56.6 us -> 56.6 us (level)
  no operation moved by 1% of the time
where the time goes in v4:
time: 56.6 us; the launch traced here: 56.4 us
  starting transfers between devices  27.5 us (49%)
  waiting for transfers between devices  19.4 us (34%)
  Pallas kernels  7.37 us (13%)
  between operations  1.38 us (2%)
  other arithmetic  0.74 us (1%)
    ppermute x4, starting transfers between devices, swapped(): return lax.ppermute(value, axis, sorted(partner.items()))  24.6 us
    ppermute x4, waiting for transfers between devices, swapped(): return lax.ppermute(value, axis, sorted(partner.items()))  15.7 us
    ppermute x3, waiting for transfers between devices, cyclic(): lax.ppermute(value, axis, [(s, (s + steps) % count) for s in range(count)])  3.75 us
    pallas_call x1, Pallas kernels, on_device(): pl.pallas_call(functools.partial(middle_kernel, sizes), out_shape=(state,...  3.02 us
    ppermute x3, starting transfers between devices, cyclic(): lax.ppermute(value, axis, [(s, (s + steps) % count) for s in range(count)])  2.92 us
    pallas_call x1, Pallas kernels, on_device(): pl.pallas_call(functools.partial(first_kernel, sizes), out_shape=(with_me...  2.42 us
    pallas_call x1, Pallas kernels, on_device(): pl.pallas_call(functools.partial(last_kernel, sizes), out_shape=(state, i...  1.93 us
  transfers between devices with their start and end apart: 7, of which 4 were waited for; matrix products, arithmetic and copies ran while one was open for 0% of the time, Pallas kernels for 0%

profile of v4, /device:TPU:33, one launch (start us, length us, event | category | flops | bytes accessed | tf_op | source)
XLA Modules:
  0.0 56.4 jit_solution(7391401372193308642)
XLA Ops:
  1.3 2.4 %first.1 = (f32[30,32,128]{2,1,0:T(8,128)S(1)}, f32[30,32,128]{2,1,0:T(8,128)S(1)}, f32[2,9,10,48,128]{4,3,2,1,0:T(8,128)S(1)}, f32[4,4,32,128]{3,2,1,0:T(8,128)...) custom-call(f32[1,2,9,4,32,128]{5,4,3,2,1,0:T(8,128)} %wavefields.1, f32[3,4,32,128]{3,2,1,0:T(8,128)} %earth.1, ...), custom_call_target="tpu_custom_call" | custom-call | flops 11796480 | bytes 1179648 | tf_op jit(solution)/shard_map/first/pallas_call | solution.py:440
  3.7 20.5 %collective-permute-start = (f32[30,32,128]{2,1,0:T(8,128)S(1)}, f32[30,32,128]{2,1,0:T(8,128)S(1)}, u32[]{:S(2)}, u32[]{:S(2)}) collective-permute-start(f32[30,32,128]{2,1,0:T(8,128)S(1)} %get-tuple-element.21), channel_id=1, source_target_pairs={{0,4},{4,0},{8,12},{12,8},{16,20},{20,16},{24,28},{28,24},{32,36},... | collective-permute-start | bytes 1474568 | tf_op jit(solution)/shard_map/ppermute | solution.py:28
  24.3 1.9 %collective-permute-start.1 = (f32[30,32,128]{2,1,0:T(8,128)S(1)}, f32[30,32,128]{2,1,0:T(8,128)S(1)}, u32[]{:S(2)}, u32[]{:S(2)}) collective-permute-start(f32[30,32,128]{2,1,0:T(8,128)S(1)} %get-tuple-element.22), channel_id=1, source_target_pairs={{0,0},{4,8},{8,4},{12,16},{16,12},{20,24},{24,20},{28,32},{32,28},... | collective-permute-start | bytes 1474568 | tf_op jit(solution)/shard_map/ppermute | solution.py:28
  26.2 0.0 collective-permute-done.chip
  26.2 8.2 %collective-permute-done.1.cross = f32[30,32,128]{2,1,0:T(8,128)S(1)} collective-permute-done((f32[30,32,128]{2,1,0:T(8,128)S(1)}, f32[30,32,128]{2,1,0:T(8,128)S(1)}, u32[]{:S(2)}, u32[]{:S(2)}) %collective-permute-start.1) | collective-permute-done | bytes 491552 | tf_op jit(solution)/shard_map/ppermute | solution.py:28
  34.4 3.0 %middle.1 = (f32[2,9,10,48,128]{4,3,2,1,0:T(8,128)S(1)}, f32[2,4,2,32,128]{4,3,2,1,0:T(8,128)S(1)}, f32[2,4,32,128]{3,2,1,0:T(8,128)S(1)}, f32[24,32,128]{2,1,0:T(8,128)S(1)}, f32[24,32,128]{2,1,0:T(8,128)S(1)}) custom-call(f32[2,9,10,48,128]{4,3,2,1,0:T(8,128)S(1)} %get-tuple-element.17.fields_in, ...), custom_call_target="tpu_custom_call", output_to_operand_aliasing={{0}: (0, {})} | custom-call | flops 29491200 | bytes 1179648 | tf_op jit(solution)/shard_map/middle/pallas_call | solution.py:458
  37.5 0.1 collective-permute-start.2
  37.6 2.0 %collective-permute-start.3 = (f32[24,32,128]{2,1,0:T(8,128)S(1)}, f32[24,32,128]{2,1,0:T(8,128)S(1)}, u32[]{:S(2)}, u32[]{:S(2)}) collective-permute-start(f32[24,32,128]{2,1,0:T(8,128)S(1)} %get-tuple-element.26), channel_id=1, source_target_pairs={{0,0},{4,8},{8,4},{12,16},{16,12},{20,24},{24,20},{28,32},{32,28},... | collective-permute-start | bytes 1179656 | tf_op jit(solution)/shard_map/ppermute | solution.py:28
  39.6 0.0 collective-permute-done.2.chip
  39.6 7.5 %collective-permute-done.3.cross = f32[24,32,128]{2,1,0:T(8,128)S(1)} collective-permute-done((f32[24,32,128]{2,1,0:T(8,128)S(1)}, f32[24,32,128]{2,1,0:T(8,128)S(1)}, u32[]{:S(2)}, u32[]{:S(2)}) %collective-permute-start.3) | collective-permute-done | bytes 393248 | tf_op jit(solution)/shard_map/ppermute | solution.py:28
  47.0 1.9 %last.1 = (f32[2,9,10,48,128]{4,3,2,1,0:T(8,128)S(1)}, f32[2,4,32,128]{3,2,1,0:T(8,128)S(1)}) custom-call(f32[2,9,10,48,128]{4,3,2,1,0:T(8,128)S(1)} %get-tuple-element.23.fields_in, f32[4,4,32,128]{3,2,1,0:T(8,128)S(1)} %get-tuple-element.18.medium, f32[2,4,2,32,128]{4,3,2,1,0:T(8,128)S(1)} %get-tuple-element.24.halo, ...), custom_call_target="tpu_custom_call", output_to_operand_aliasing={{0}: (0, {})} | custom-call | flops 17694720 | bytes 1179648 | tf_op jit(solution)/shard_map/last/pallas_call | solution.py:469
  49.0 0.1 collective-permute-start.4
  49.1 0.1 collective-permute-start.5
  49.2 2.6 %collective-permute-start.6 = (f32[2,4,32,128]{3,2,1,0:T(8,128)S(1)}, f32[2,4,32,128]{3,2,1,0:T(8,128)S(1)}, u32[]{:S(2)}, u32[]{:S(2)}) collective-permute-start(f32[2,4,32,128]{3,2,1,0:T(8,128)S(1)} %get-tuple-element.28), channel_id=1, source_target_pairs={{0,3},{1,0},{2,1},{3,2},{4,7},{5,4},{6,5},{7,6},{8,11},{9,8},{10,9... | collective-permute-start | bytes 393224 | tf_op jit(solution)/shard_map/ppermute | solution.py:20
  51.9 2.6 %collective-permute-done.4 = f32[2,4,32,128]{3,2,1,0:T(8,128)S(1)} collective-permute-done((f32[2,4,32,128]{3,2,1,0:T(8,128)S(1)}, f32[2,4,32,128]{3,2,1,0:T(8,128)S(1)}, u32[]{:S(2)}, u32[]{:S(2)}) %collective-permute-start.4) | collective-permute-done | bytes 131104 | tf_op jit(solution)/shard_map/ppermute | solution.py:20
  54.5 1.1 %collective-permute-done.5 = f32[2,4,32,128]{3,2,1,0:T(8,128)S(1)} collective-permute-done((f32[2,4,32,128]{3,2,1,0:T(8,128)S(1)}, f32[2,4,32,128]{3,2,1,0:T(8,128)S(1)}, u32[]{:S(2)}, u32[]{:S(2)}) %collective-permute-start.5) | collective-permute-done | bytes 131104 | tf_op jit(solution)/shard_map/ppermute | solution.py:20
  55.7 0.0 collective-permute-done.6
  55.7 0.7 %add_multiply_fusion = f32[2,4,32,128]{3,2,1,0:T(8,128)} fusion(f32[2,4,32,128]{3,2,1,0:T(8,128)S(1)} %collective-permute-done.6, f32[2,4,32,128]{3,2,1,0:T(8,128)S(1)} %collective-permute-done.5, f32[2,4,32,128]{3,2,1,0:T(8,128)S(1)} %get-tuple-element.28, f32[2,4,32,128]{3,2,1,0:T(8,128)S(1)} %collective-permute-done.4, f32[2]{0:T(128)S(1)} %compare_select_fusion), kind=kLoop, calls=%fused_computation | loop fusion | flops 131072 | bytes 655368 | tf_op jit(solution)/shard_map/mul | solution.py:484
  (1 shorter events, 0.0 us)
Async XLA Ops:
  3.7 22.5 %collective-permute-start = (f32[30,32,128]{2,1,0:T(8,128)S(1)}, f32[30,32,128]{2,1,0:T(8,128)S(1)}, u32[]{:S(2)}, u32[]{:S(2)}) collective-permute-start(f32[30,32,128]{2,1,0:T(8,128)S(1)} %get-tuple-element.21), channel_id=1, source_target_pairs={{0,4},{4,0},{8,12},{12,8},{16,20},{20,16},{24,28},{28,24},{32,36},... | collective-permute-start | bytes 1474568 | tf_op jit(solution)/shard_map/ppermute | solution.py:28
  24.3 10.2 %collective-permute-start.1 = (f32[30,32,128]{2,1,0:T(8,128)S(1)}, f32[30,32,128]{2,1,0:T(8,128)S(1)}, u32[]{:S(2)}, u32[]{:S(2)}) collective-permute-start(f32[30,32,128]{2,1,0:T(8,128)S(1)} %get-tuple-element.22), channel_id=1, source_target_pairs={{0,0},{4,8},{8,4},{12,16},{16,12},{20,24},{24,20},{28,32},{32,28},... | collective-permute-start | bytes 1474568 | tf_op jit(solution)/shard_map/ppermute | solution.py:28
  37.5 2.1 %collective-permute-start.2 = (f32[24,32,128]{2,1,0:T(8,128)S(1)}, f32[24,32,128]{2,1,0:T(8,128)S(1)}, u32[]{:S(2)}, u32[]{:S(2)}) collective-permute-start(f32[24,32,128]{2,1,0:T(8,128)S(1)} %get-tuple-element.25), channel_id=1, source_target_pairs={{0,4},{4,0},{8,12},{12,8},{16,20},{20,16},{24,28},{28,24},{32,36},... | collective-permute-start | bytes 1179656 | tf_op jit(solution)/shard_map/ppermute | solution.py:28
  37.6 9.4 %collective-permute-start.3 = (f32[24,32,128]{2,1,0:T(8,128)S(1)}, f32[24,32,128]{2,1,0:T(8,128)S(1)}, u32[]{:S(2)}, u32[]{:S(2)}) collective-permute-start(f32[24,32,128]{2,1,0:T(8,128)S(1)} %get-tuple-element.26), channel_id=1, source_target_pairs={{0,0},{4,8},{8,4},{12,16},{16,12},{20,24},{24,20},{28,32},{32,28},... | collective-permute-start | bytes 1179656 | tf_op jit(solution)/shard_map/ppermute | solution.py:28
  49.0 5.5 %collective-permute-start.4 = (f32[2,4,32,128]{3,2,1,0:T(8,128)S(1)}, f32[2,4,32,128]{3,2,1,0:T(8,128)S(1)}, u32[]{:S(2)}, u32[]{:S(2)}) collective-permute-start(f32[2,4,32,128]{3,2,1,0:T(8,128)S(1)} %get-tuple-element.28), channel_id=1, source_target_pairs={{0,2},{1,3},{2,0},{3,1},{4,6},{5,7},{6,4},{7,5},{8,10},{9,11},{10,... | collective-permute-start | bytes 393224 | tf_op jit(solution)/shard_map/ppermute | solution.py:20
  49.1 6.5 %collective-permute-start.5 = (f32[2,4,32,128]{3,2,1,0:T(8,128)S(1)}, f32[2,4,32,128]{3,2,1,0:T(8,128)S(1)}, u32[]{:S(2)}, u32[]{:S(2)}) collective-permute-start(f32[2,4,32,128]{3,2,1,0:T(8,128)S(1)} %get-tuple-element.28), channel_id=1, source_target_pairs={{0,1},{1,2},{2,3},{3,0},{4,5},{5,6},{6,7},{7,4},{8,9},{9,10},{10,1... | collective-permute-start | bytes 393224 | tf_op jit(solution)/shard_map/ppermute | solution.py:20
  49.2 6.4 %collective-permute-start.6 = (f32[2,4,32,128]{3,2,1,0:T(8,128)S(1)}, f32[2,4,32,128]{3,2,1,0:T(8,128)S(1)}, u32[]{:S(2)}, u32[]{:S(2)}) collective-permute-start(f32[2,4,32,128]{3,2,1,0:T(8,128)S(1)} %get-tuple-element.28), channel_id=1, source_target_pairs={{0,3},{1,0},{2,1},{3,2},{4,7},{5,4},{6,5},{7,6},{8,11},{9,8},{10,9... | collective-permute-start | bytes 393224 | tf_op jit(solution)/shard_map/ppermute | solution.py:20
